TPU v7x, 16 devices: a whole 2x2x2 slice. The times are simulated.
16 devices in a mesh: dp: 4 (over z, y), tp: 4 (over x, core).
Axes of the slice: x: 2, y: 2, z: 2, core: 2. Of those that a mesh axis runs over, the one named last changes fastest.
Arguments:
- hidden: bfloat16 [8, 1024, 2048], P('dp', 'tp'), parts along dimension 0
- positions: int32 [8, 1024], P('dp'), parts along dimension 0
- norm_w: float32 [2048], replicated
- w_query: bfloat16 [2048, 2048], P(None, 'tp')
- w_key: bfloat16 [2048, 128], replicated
- w_value: bfloat16 [2048, 128], replicated
- w_out: bfloat16 [2048, 2048], P('tp')
- grad_out: bfloat16 [8, 1024, 2048], P('dp', 'tp'), parts along dimension 0
Outputs:
- output 1: bfloat16 [8, 1024, 2048], P('dp', 'tp'), parts along dimension 0
- output 2: bfloat16 [8, 1024, 2048], P('dp', 'tp'), parts along dimension 0
- output 3: float32 [8192, 2048], P('dp', 'tp'), parts along dimension 0
- output 4: float32 [8192, 2048], P(('dp', 'tp')), parts along dimension 0
- output 5: float32 [8192, 128], P('dp'), parts along dimension 0
- output 6: float32 [8192, 128], P('dp'), parts along dimension 0
- output 7: float32 [8192], P('dp'), parts along dimension 0
There are 4 independent parts. A program takes and returns all parts, laid end to end along the dimension named above; an argument that names none is the same for every part.
All inputs are finite; a program needn't handle non-finite values.
Results may differ from a plain program's by a relative error of at most 0.02.
Values are sent between devices in bfloat16 or wider.
A program may use at most 1 GiB of HBM per device.

v0:
```python
import jax
import jax.numpy as jnp
from jax import lax
from jax.sharding import PartitionSpec as P


def rope_tables(positions, head_dim):
    half = head_dim // 2
    inv_freq = 10000.0 ** (-2.0 * jnp.arange(half, dtype=jnp.float32) / head_dim)
    angle = positions.astype(jnp.float32)[..., None] * inv_freq
    return jnp.cos(angle), jnp.sin(angle)


def apply_rope(vector, cos_t, sin_t):
    half = vector.shape[-1] // 2
    first = vector[..., :half]
    second = vector[..., half:]
    return jnp.concatenate([first * cos_t - second * sin_t, second * cos_t + first * sin_t], axis=-1)


def local_block(hidden, positions, norm_w, w_query, w_key, w_value, w_out, grad_out):
    batch = hidden.shape[0]
    seq_len = positions.shape[1]
    head_dim = w_key.shape[1]
    heads_dev = w_query.shape[1] // head_dim
    scale = head_dim ** -0.5
    hidden_f = hidden.astype(jnp.float32)
    inv_rms = lax.rsqrt(jnp.mean(hidden_f * hidden_f, axis=-1, keepdims=True) + 1e-6)
    normed = hidden_f * inv_rms
    gain = 1.0 + norm_w
    act_local = (normed * gain).astype(jnp.bfloat16)
    act_full = lax.all_gather(act_local, 'tp', axis=1, tiled=True)
    query = jnp.einsum('bsd,de->bse', act_full, w_query, preferred_element_type=jnp.float32).astype(jnp.bfloat16).reshape(batch, seq_len, heads_dev, head_dim)
    key_proj = jnp.einsum('bsd,de->bse', act_full, w_key, preferred_element_type=jnp.float32).astype(jnp.bfloat16)
    value_proj = jnp.einsum('bsd,de->bse', act_full, w_value, preferred_element_type=jnp.float32).astype(jnp.bfloat16)
    cos_t, sin_t = rope_tables(positions, head_dim)
    cos_h = cos_t[:, :, None]
    sin_h = sin_t[:, :, None]
    q_rot = (apply_rope(query.astype(jnp.float32), cos_h, sin_h) * scale).astype(jnp.bfloat16)
    k_rot = apply_rope(key_proj.astype(jnp.float32), cos_t, sin_t).astype(jnp.bfloat16)
    scores = jnp.einsum('crie,cle->cirl', q_rot, k_rot, preferred_element_type=jnp.float32)
    causal = jnp.arange(seq_len)[:, None] >= jnp.arange(seq_len)[None, :]
    attn_probs = jax.nn.softmax(jnp.where(causal, scores, -1e30), axis=-1)
    probs_low = attn_probs.astype(jnp.bfloat16)
    attended = jnp.einsum('cirl,cle->crie', probs_low, value_proj, preferred_element_type=jnp.float32).astype(jnp.bfloat16).reshape(batch, seq_len, heads_dev * head_dim)
    out_part = jnp.einsum('bse,ed->bsd', attended, w_out, preferred_element_type=jnp.float32).astype(jnp.bfloat16)
    out_local = lax.psum_scatter(out_part, 'tp', scatter_dimension=1, tiled=True)
    output = (hidden_f + out_local.astype(jnp.float32)).astype(jnp.bfloat16)

    grad_full = lax.all_gather(grad_out, 'tp', axis=1, tiled=True)
    grad_w_out = jnp.einsum('bse,bsd->ed', attended, grad_full, preferred_element_type=jnp.float32)
    grad_att = jnp.einsum('bsd,ed->bse', grad_full, w_out, preferred_element_type=jnp.float32).astype(jnp.bfloat16).reshape(batch, seq_len, heads_dev, head_dim)
    grad_value = jnp.einsum('cirl,crie->cle', probs_low, grad_att, preferred_element_type=jnp.float32).astype(jnp.bfloat16)
    grad_probs = jnp.einsum('crie,cle->cirl', grad_att, value_proj, preferred_element_type=jnp.float32)
    row_dot = jnp.sum(grad_probs * attn_probs, axis=-1, keepdims=True)
    grad_scores = (attn_probs * (grad_probs - row_dot)).astype(jnp.bfloat16)
    grad_qrot = jnp.einsum('cirl,cle->crie', grad_scores, k_rot, preferred_element_type=jnp.float32)
    grad_krot = jnp.einsum('cirl,crie->cle', grad_scores, q_rot, preferred_element_type=jnp.float32)
    grad_query = apply_rope(grad_qrot * scale, cos_h, -sin_h).astype(jnp.bfloat16).reshape(batch, seq_len, heads_dev * head_dim)
    grad_key = apply_rope(grad_krot, cos_t, -sin_t).astype(jnp.bfloat16)
    grad_w_query = jnp.einsum('bsd,bse->de', act_full, grad_query, preferred_element_type=jnp.float32)
    grad_w_key = jnp.einsum('bsd,bse->de', act_full, grad_key, preferred_element_type=jnp.float32)
    grad_w_value = jnp.einsum('bsd,bse->de', act_full, grad_value, preferred_element_type=jnp.float32)
    grad_w_key, grad_w_value = lax.psum((grad_w_key, grad_w_value), 'tp')
    grad_act_part = (jnp.einsum('bse,de->bsd', grad_query, w_query, preferred_element_type=jnp.float32)
                     + jnp.einsum('bse,de->bsd', grad_key, w_key, preferred_element_type=jnp.float32)
                     + jnp.einsum('bse,de->bsd', grad_value, w_value, preferred_element_type=jnp.float32)).astype(jnp.bfloat16)
    grad_act = lax.psum_scatter(grad_act_part, 'tp', scatter_dimension=1, tiled=True).astype(jnp.float32)
    grad_norm_part = jnp.sum(grad_act * normed, axis=(0, 1))
    grad_normed = grad_act * gain
    grad_hidden = (grad_out.astype(jnp.float32) + inv_rms * (grad_normed - normed * jnp.mean(grad_normed * normed, axis=-1, keepdims=True))).astype(jnp.bfloat16)
    grad_norm_w = lax.psum(grad_norm_part, 'tp')
    return output, grad_hidden, grad_w_query, grad_w_out, grad_w_key, grad_w_value, grad_norm_w


def solution(mesh):
    specs_in = (P('dp', 'tp', None), P('dp', None), P(None), P(None, 'tp'), P(None, None), P(None, None), P('tp', None), P('dp', 'tp', None))
    specs_out = (P('dp', 'tp', None), P('dp', 'tp', None), P('dp', 'tp'), P(('dp', 'tp'), None), P('dp', None), P('dp', None), P('dp'))
    return jax.shard_map(local_block, mesh=mesh, in_specs=specs_in, out_specs=specs_out, check_vma=False)
```

profile of v0, /device:TPU:0, one launch (start us, length us, event | category | flops | bytes accessed | tf_op | source)
XLA Modules:
  0.0 486.3 jit_solution(9433152238096796669)
XLA Ops:
  7.2 2.2 fusion.22
  9.5 0.7 broadcast_add_fusion
  10.8 3.5 fusion.19
  14.4 0.7 all-gather.5.cloned.1.call-update
  15.2 1.3 iota_compare_fusion
  16.4 57.5 %all-gather.3.cloned.1.call-done = bf16[2,1024,2048]{2,1,0:T(8,128)(2,1)} async-done(((bf16[2,256,2048]{2,1,0:T(8,128)(2,1)}), bf16[2,1024,2048]{2,1,0:T(8,128)(2,1)}) %all-gather.3.cloned.1.call-update) | async-done | bytes 8388624 | tf_op jit(solution)/shard_map/all_gather | solution.py:32
  73.9 6.3 %fusion.49 = f32[2,1024,128]{1,2,0:T(8,128)S(1)} fusion(bf16[2,1024,2048]{2,1,0:T(8,128)(2,1)} %all-gather.3.cloned.1.call-done, bf16[2048,128]{1,0:T(8,128)(2,1)S(1)} %copy-done.3), kind=kOutput, calls=%fused_computation.63 | convolution fusion | flops 1074266112 | bytes 9961472 | tf_op jit(solution)/shard_map/bsd,de->bse/dot_general | solution.py:34
  80.2 3.1 fusion.59
  83.3 1.3 copy.42
  84.6 1.4 copy.40
  86.0 8.6 %fusion.34 = bf16[2,1024,512]{1,2,0:T(8,128)(2,1)S(1)} fusion(bf16[2,1024,2048]{2,1,0:T(8,128)(2,1)} %all-gather.3.cloned.1.call-done, bf16[2048,512]{1,0:T(8,128)(2,1)S(1)} %copy-done), kind=kOutput, calls=%fused_computation.56 | convolution fusion | flops 4296015872 | bytes 12582912 | tf_op jit(solution)/shard_map/bsd,de->bse/dot_general | solution.py:33
  94.6 2.5 fusion.80
  97.1 3.8 copy.92
  101.0 3.8 copy.91
  104.8 5.1 %multiply_subtract_fusion = (f32[2,1024,4,64]{3,1,2,0:T(8,128)S(1)}, f32[2,1024,4,64]{3,1,2,0:T(8,128)S(1)}) fusion(f32[2,1024,4,64]{3,1,2,0:T(8,128)} %copy.92, f32[2,1024,4,64]{3,1,2,0:T(8,128)} %copy.91, f32[2,1024,64]{2,1,0:T(8,128)} %copy.42, f32[2,1024,64]{2,1,0:T(8,128)S(1)} %copy.40), kind=kLoop, calls=%fused_computation.41 | loop fusion | flops 3145728 | bytes 9437184 | tf_op jit(solution)/shard_map/sub | solution.py:18
  109.9 2.5 fusion.24
  112.4 19.3 %fusion.81 = (f32[2,4,1024]{2,1,0:T(4,128)S(1)}, f32[2,4,1024,1024]{2,3,1,0:T(8,128)}) fusion(pred[1024,1024]{0,1:T(8,128)(4,1)} %iota_compare_fusion, bf16[2,1024,4,128]{3,1,2,0:T(8,128)(2,1)} %fusion.24, bf16[2,1024,64]{1,2,0:T(8,128)(2,1)S(1)} %copy-done.7, bf16[2,1024,64]{1,2,0:T(8,128)(2,1)S(1)} %get-tuple-element.21), kind=kOutput, calls=%fused_computation.102 | convolution fusion | flops 2173699072 | bytes 37257216 | tf_op jit(solution)/shard_map/sub | solution.py:43
  132.1 8.5 %fusion.37 = bf16[2,1024,512]{1,2,0:T(8,128)(2,1)S(1)} fusion(bf16[2,1024,2048]{2,1,0:T(8,128)(2,1)} %all-gather.5.cloned.1.call-done, bf16[512,2048]{1,0:T(8,128)(2,1)} %param.14), kind=kOutput, calls=%fused_computation.57 | convolution fusion | flops 4296015872 | bytes 12582912 | tf_op jit(solution)/shard_map/bsd,ed->bse/dot_general | solution.py:52
  140.6 14.1 %fusion.46 = bf16[2,1024,128]{2,1,0:T(8,128)(2,1)} fusion(bf16[2,1024,4,128]{1,3,2,0:T(8,128)(2,1)S(1)} %bitcast.124, f32[2,4,1024,1024]{2,3,1,0:T(8,128)} %get-tuple-element.27, f32[2,4,1024]{2,1,0:T(4,128)S(1)} %get-tuple-element.26), kind=kOutput, calls=%fused_computation.61 | convolution fusion | flops 2164523008 | bytes 36208640 | tf_op jit(solution)/shard_map/cirl,crie->cle/dot_general | solution.py:53
  154.8 5.7 %fusion.50 = bf16[2,1024,128,1]{2,1,3,0:T(8,128)(2,1)S(1)} fusion(bf16[2,1024,2048]{2,1,0:T(8,128)(2,1)} %all-gather.3.cloned.1.call-done, bf16[2048,128]{1,0:T(8,128)(2,1)S(1)} %copy-done.8), kind=kOutput, calls=%fused_computation.65 | convolution fusion | flops 1074003968 | bytes 9437184 | tf_op jit(solution)/shard_map/bsd,de->bse/dot_general | solution.py:35
  160.6 24.8 %fusion.1 = (f32[2,4,1024]{2,1,0:T(4,128)S(1)}, f32[2,1024,1024,4]{2,1,3,0:T(8,128)}) fusion(f32[2,4,1024,1024]{2,3,1,0:T(8,128)} %get-tuple-element.27, f32[2,4,1024]{2,1,0:T(4,128)S(1)} %get-tuple-element.26, bf16[2,1024,128,1]{2,1,3,0:T(8,128)(2,1)S(1)} %fusion.50, bf16[2,1024,4,128]{1,3,2,0:T(8,128)(2,1)S(1)} %bitcast.125), kind=kOutput, calls=%fused_computation.3 | convolution fusion | flops 2172641280 | bytes 69795840 | tf_op jit(solution)/shard_map/crie,cle->cirl/dot_general | solution.py:54
  185.4 27.9 %fusion.3 = bf16[2,4,1024,1024]{2,3,1,0:T(8,128)(2,1)} fusion(f32[2,1024,1024,4]{2,1,3,0:T(8,128)} %get-tuple-element.29, f32[2,4,1024]{2,1,0:T(4,128)S(1)} %get-tuple-element.28, f32[2,4,1024,1024]{2,3,1,0:T(8,128)} %get-tuple-element.27, f32[2,4,1024]{2,1,0:T(4,128)S(1)} %get-tuple-element.26), kind=kLoop, calls=%fused_computation.5 | loop fusion | flops 33554432 | bytes 83951616 | tf_op jit(solution)/shard_map/convert_element_type | solution.py:56
  213.3 10.6 %convolution_bitcast_fusion.4 = f32[2,1024,128]{1,2,0:T(8,128)} fusion(bf16[2,4,1024,1024]{2,3,1,0:T(8,128)(2,1)} %fusion.3, bf16[2,1024,4,128]{3,1,2,0:T(8,128)(2,1)} %fusion.24), kind=kOutput, calls=%fused_computation.60 | convolution fusion | flops 2147483648 | bytes 19922944 | tf_op jit(solution)/shard_map/cirl,crie->cle/dot_general | solution.py:58
  223.9 12.7 %multiply_bitcast_fusion = f32[2,1024,4,128]{3,1,2,0:T(8,128)} fusion(bf16[2,4,1024,1024]{2,3,1,0:T(8,128)(2,1)} %fusion.3, bf16[2,1024,64]{1,2,0:T(8,128)(2,1)S(1)} %copy-done.7, bf16[2,1024,64]{1,2,0:T(8,128)(2,1)S(1)} %get-tuple-element.21), kind=kOutput, calls=%fused_computation.39 | convolution fusion | flops 2149580800 | bytes 21495808 | tf_op jit(solution)/shard_map/cirl,cle->crie/dot_general | solution.py:57
  236.6 4.0 fusion.63
  240.7 2.4 copy.50
  243.0 5.0 %subtract_convert_fusion = (bf16[2,1024,4,64]{3,1,2,0:T(8,128)(2,1)S(1)}, bf16[2,1024,4,64]{3,1,2,0:T(8,128)(2,1)S(1)}) fusion(f32[2,1024,4,128]{3,1,2,0:T(8,128)} %multiply_bitcast_fusion, f32[2,1024,64]{2,1,0:T(8,128)} %copy.50, f32[2,1024,64]{2,1,0:T(8,128)S(1)} %copy-done.2), kind=kLoop, calls=%fused_computation.38 | loop fusion | flops 4194304 | bytes 7340032 | tf_op jit(solution)/shard_map/convert.3
  248.0 2.5 pad_maximum_fusion
  250.5 3.9 copy.51
  254.4 9.9 %fusion.30 = f32[2,1024,2048]{2,1,0:T(8,128)} fusion(bf16[2,1024,512]{1,2,0:T(8,128)(2,1)} %bitcast.120, bf16[2048,512]{1,0:T(8,128)(2,1)S(1)} %copy-done), kind=kOutput, calls=%fused_computation.52 | convolution fusion | flops 4294967296 | bytes 20971520 | tf_op jit(solution)/shard_map/bse,de->bsd/dot_general | solution.py:65
  264.3 8.1 %fusion.66 = f32[2,1024,2048]{2,1,0:T(8,128)} fusion(bf16[2048,128]{1,0:T(8,128)(2,1)S(1)} %copy-done.4, bf16[2,1024,64]{1,2,0:T(8,128)(2,1)S(1)} %copy-done.6, bf16[2,1024,64]{1,2,0:T(8,128)(2,1)S(1)} %get-tuple-element.19), kind=kOutput, calls=%fused_computation.85 | convolution fusion | flops 1074790400 | bytes 17825792 | tf_op jit(solution)/shard_map/bse,de->bsd/dot_general | solution.py:66
  272.4 15.5 %add_convert_fusion = bf16[2,1024,2048]{2,1,0:T(8,128)(2,1)} fusion(f32[2,1024,2048]{2,1,0:T(8,128)} %fusion.30, f32[2,1024,2048]{2,1,0:T(8,128)} %fusion.66, bf16[2,1024,128]{2,1,0:T(8,128)(2,1)} %fusion.46, bf16[2048,128]{1,0:T(8,128)(2,1)S(1)} %copy-done.9), kind=kOutput, calls=%fused_computation.9 | convolution fusion | flops 1086324736 | bytes 42991616 | tf_op jit(solution)/shard_map/bse,de->bsd/dot_general | solution.py:67
  288.0 1.0 copy-done.23
  289.0 12.4 %fusion.40 = bf16[2,128,4,1024]{3,1,2,0:T(8,128)(2,1)S(1)} fusion(bf16[2,1024,128,1]{2,1,3,0:T(8,128)(2,1)S(1)} %copy-done.23, f32[2,4,1024,1024]{2,3,1,0:T(8,128)} %get-tuple-element.27, f32[2,4,1024]{2,1,0:T(4,128)S(1)} %get-tuple-element.26), kind=kOutput, calls=%fused_computation.58 | convolution fusion | flops 2165309440 | bytes 36208640 | tf_op jit(solution)/shard_map/cirl,cle->crie/dot_general | solution.py:45
  301.4 1.3 copy-done.21
  302.7 6.8 %convolution_convert_fusion = bf16[2,1024,2048]{2,1,0:T(8,128)(2,1)} fusion(bf16[2,1024,512]{1,2,0:T(8,128)(2,1)S(1)} %bitcast.122, bf16[512,2048]{1,0:T(8,128)(2,1)S(1)} %copy-done.20), kind=kOutput, calls=%fused_computation.24 | convolution fusion | flops 4299161600 | bytes 12582912 | tf_op jit(solution)/shard_map/bse,ed->bsd/dot_general | solution.py:46
  309.7 6.8 %convolution_bitcast_fusion.3 = f32[2048,128]{1,0:T(8,128)} fusion(bf16[2,1024,2048]{2,1,0:T(8,128)(2,1)} %all-gather.3.cloned.1.call-done, bf16[2,1024,64]{1,2,0:T(8,128)(2,1)S(1)} %copy-done.6, bf16[2,1024,64]{1,2,0:T(8,128)(2,1)S(1)} %get-tuple-element.19), kind=kOutput, calls=%fused_computation.47 | convolution fusion | flops 1074790400 | bytes 9961472 | tf_op jit(solution)/shard_map/bsd,bse->de/dot_general | solution.py:62
  316.4 6.7 %convolution_bitcast_fusion.2 = f32[2048,128]{1,0:T(8,128)} fusion(bf16[2,1024,2048]{2,1,0:T(8,128)(2,1)} %all-gather.3.cloned.1.call-done, bf16[2,1024,128]{2,1,0:T(8,128)(2,1)S(1)} %copy-done.10), kind=kOutput, calls=%fused_computation.46 | convolution fusion | flops 1073741824 | bytes 9961472 | tf_op jit(solution)/shard_map/bsd,bse->de/dot_general | solution.py:63
  323.2 10.7 %convolution_bitcast_fusion = f32[512,2048]{1,0:T(8,128)} fusion(bf16[2,1024,512]{1,2,0:T(8,128)(2,1)} %bitcast.123, bf16[2,1024,2048]{2,1,0:T(8,128)(2,1)} %all-gather.5.cloned.1.call-done), kind=kOutput, calls=%fused_computation.44 | convolution fusion | flops 4294967296 | bytes 14680064 | tf_op jit(solution)/shard_map/bse,bsd->ed/dot_general | solution.py:51
  333.9 10.0 %convolution_bitcast_fusion.1 = f32[2048,512]{1,0:T(8,128)} fusion(bf16[2,1024,2048]{2,1,0:T(8,128)(2,1)} %all-gather.3.cloned.1.call-done, bf16[2,1024,512]{1,2,0:T(8,128)(2,1)S(1)} %bitcast.121), kind=kOutput, calls=%fused_computation.45 | convolution fusion | flops 4294967296 | bytes 14680064 | tf_op jit(solution)/shard_map/bsd,bse->de/dot_general | solution.py:61
  343.9 11.2 %reduce-scatter.5.cloned.1.call-done = bf16[2,256,2048]{2,1,0:T(8,128)(2,1)} async-done(((bf16[2,1024,2048]{2,1,0:T(8,128)(2,1)}), bf16[2,256,2048]{2,1,0:T(8,128)(2,1)}) %reduce-scatter.5.cloned.1.call-update) | async-done | bytes 2097168 | tf_op jit(solution)/shard_map/reduce_scatter | solution.py:68
  355.1 3.8 fusion.21
  358.9 6.4 %psum.23 = f32[2048]{0:T(1024)} all-reduce(f32[2048]{0:T(1024)S(1)} %get-tuple-element.7), channel_id=1, replica_groups=mesh['dp'=4,'tp'=4] {'tp'}, use_global_device_ids=true, to_apply=%region_10.11 | all-reduce | flops 2048 | bytes 16384 | tf_op jit(solution)/shard_map/psum | solution.py:72
  365.3 59.1 %reduce-scatter.3.cloned.1.call-done = bf16[2,256,2048]{2,1,0:T(8,128)(2,1)} async-done(((bf16[2,1024,2048]{2,1,0:T(8,128)(2,1)}), bf16[2,256,2048]{2,1,0:T(8,128)(2,1)}) %reduce-scatter.3.cloned.1.call-update) | async-done | bytes 2097168 | tf_op jit(solution)/shard_map/reduce_scatter | solution.py:47
  424.4 6.0 %fusion.18 = (bf16[2,256,2048]{2,1,0:T(8,128)(2,1)}, bf16[2,256,2048]{2,1,0:T(8,128)(2,1)}) fusion(bf16[2,256,2048]{2,1,0:T(8,128)(2,1)} %reduce-scatter.5.cloned.1.call-done, bf16[2,256,2048]{2,1,0:T(8,128)(2,1)} %param.8, bf16[2,256,2048]{2,1,0:T(8,128)(2,1)} %param.15, f32[2,256]{1,0:T(2,128)S(1)} %broadcast_multiply_fusion, f32[2048]{0:T(1024)S(1)} %copy-done.12, ...), kind=kLoop, calls=%fused_computation.29 | loop fusion | flops 13631488 | bytes 12595200 | tf_op jit(solution)/shard_map/convert_element_type | solution.py:71
  430.4 44.4 %all-reduce.3.cloned.1.call-done = (f32[2048,128]{1,0:T(8,128)}, f32[2048,128]{1,0:T(8,128)}) async-done(((f32[2048,128]{1,0:T(8,128)}, f32[2048,128]{1,0:T(8,128)}), (f32[2048,128]{1,0:T(8,128)}, f32[2048,128]{1,0:T(8,128)})) %all-reduce.3.cloned.1.call-update) | async-done | bytes 2097168 | tf_op jit(solution)/shard_map/psum | solution.py:64
  474.8 2.3 copy.95
  477.1 2.3 copy.96
  (60 shorter events, 1.4 us)
Async XLA Ops:
  7.2 78.8 %copy-start = (bf16[2048,512]{1,0:T(8,128)(2,1)S(1)}, bf16[2048,512]{1,0:T(8,128)(2,1)}, u32[]{:S(2)}) copy-start(bf16[2048,512]{1,0:T(8,128)(2,1)} %param.11) | copy-start | bytes 6291460
  7.2 66.7 %all-gather.3.cloned.1.call-start = ((), (), s32[]{:S(2)}) async-start(), calls=%async_computation.2 | async-start | bytes 10485760 | tf_op jit(solution)/shard_map/all_gather | solution.py:32
  9.5 0.7 copy-start.15
  10.2 0.6 copy-start.11
  10.8 4.3 copy-start.17
  10.8 63.2 %copy-start.3 = (bf16[2048,128]{1,0:T(8,128)(2,1)S(1)}, bf16[2048,128]{1,0:T(8,128)(2,1)}, u32[]{:S(2)}) copy-start(bf16[2048,128]{1,0:T(8,128)(2,1)} %param.12) | copy-start | bytes 1572868
  14.3 117.8 %all-gather.5.cloned.1.call-start = ((), (), s32[]{:S(2)}) async-start(), calls=%async_computation.4 | async-start | bytes 10485760 | tf_op jit(solution)/shard_map/all_gather | solution.py:50
  15.1 340.0 %reduce-scatter.5.cloned.1.call-start = ((), (), s32[]{:S(2)}) async-start(), calls=%async_computation.5 | async-start | bytes 10485760 | tf_op jit(solution)/shard_map/reduce_scatter | solution.py:68
  15.1 65.1 %copy-start.13 = (f32[2,1024]{1,0:T(2,128)}, f32[2,1024]{1,0:T(2,128)S(1)}, u32[]{:S(2)}) copy-start(f32[2,1024]{1,0:T(2,128)S(1)} %convert_element_type.81) | copy-start | bytes 24580
  15.2 65.1 %copy-start.18 = (f32[64]{0:T(128)}, f32[64]{0:T(128)S(1)}, u32[]{:S(2)}) copy-start(f32[64]{0:T(128)S(1)} %multiply_power_fusion) | copy-start | bytes 772
  86.0 18.8 %copy-start.1 = (f32[2,1024,64]{2,1,0:T(8,128)}, f32[2,1024,64]{2,1,0:T(8,128)S(1)}, u32[]{:S(2)}) copy-start(f32[2,1024,64]{2,1,0:T(8,128)S(1)} %copy.40) | copy-start | bytes 1572868
  109.9 2.5 copy-start.7
  140.6 14.2 %copy-start.8 = (bf16[2048,128]{1,0:T(8,128)(2,1)S(1)}, bf16[2048,128]{1,0:T(8,128)(2,1)}, u32[]{:S(2)}) copy-start(bf16[2048,128]{1,0:T(8,128)(2,1)} %param.13) | copy-start | bytes 1572868
  160.5 24.9 %copy-start.22 = (bf16[2,1024,128,1]{2,1,3,0:T(8,128)(2,1)}, bf16[2,1024,128,1]{2,1,3,0:T(8,128)(2,1)S(1)}, u32[]{:S(2)}) copy-start(bf16[2,1024,128,1]{2,1,3,0:T(8,128)(2,1)S(1)} %fusion.50) | copy-start | bytes 1572868
  223.9 12.7 %copy-start.14 = (f32[2,1024]{1,0:T(2,128)S(1)}, f32[2,1024]{1,0:T(2,128)}, u32[]{:S(2)}) copy-start(f32[2,1024]{1,0:T(2,128)} %copy-done.13) | copy-start | bytes 24580
  223.9 12.7 %copy-start.19 = (f32[64]{0:T(128)S(1)}, f32[64]{0:T(128)}, u32[]{:S(2)}) copy-start(f32[64]{0:T(128)} %copy-done.18) | copy-start | bytes 772
  236.6 6.4 %copy-start.2 = (f32[2,1024,64]{2,1,0:T(8,128)S(1)}, f32[2,1024,64]{2,1,0:T(8,128)}, u32[]{:S(2)}) copy-start(f32[2,1024,64]{2,1,0:T(8,128)} %copy-done.1) | copy-start | bytes 1572868
  254.4 9.9 %copy-start.4 = (bf16[2048,128]{1,0:T(8,128)(2,1)S(1)}, bf16[2048,128]{1,0:T(8,128)(2,1)}, u32[]{:S(2)}) copy-start(bf16[2048,128]{1,0:T(8,128)(2,1)} %param.12) | copy-start | bytes 1572868
  254.4 9.9 %copy-start.6 = (bf16[2,1024,64]{1,2,0:T(8,128)(2,1)S(1)}, bf16[2,1024,64]{1,2,0:T(8,128)(2,1)}, u32[]{:S(2)}) copy-start(bf16[2,1024,64]{1,2,0:T(8,128)(2,1)} %get-tuple-element.20) | copy-start | bytes 786436
  264.3 8.1 %copy-start.9 = (bf16[2048,128]{1,0:T(8,128)(2,1)S(1)}, bf16[2048,128]{1,0:T(8,128)(2,1)}, u32[]{:S(2)}) copy-start(bf16[2048,128]{1,0:T(8,128)(2,1)} %param.13) | copy-start | bytes 1572868
  288.0 1.0 copy-start.23
  288.0 136.4 %reduce-scatter.3.cloned.1.call-start = ((), (), s32[]{:S(2)}) async-start(), calls=%async_computation.3 | async-start | bytes 10485760 | tf_op jit(solution)/shard_map/reduce_scatter | solution.py:47
  289.0 13.7 %copy-start.20 = (bf16[512,2048]{1,0:T(8,128)(2,1)S(1)}, bf16[512,2048]{1,0:T(8,128)(2,1)}, u32[]{:S(2)}) copy-start(bf16[512,2048]{1,0:T(8,128)(2,1)} %param.14) | copy-start | bytes 6291460
  301.4 1.3 copy-start.21
  309.6 6.9 %copy-start.10 = (bf16[2,1024,128]{2,1,0:T(8,128)(2,1)S(1)}, bf16[2,1024,128]{2,1,0:T(8,128)(2,1)}, u32[]{:S(2)}) copy-start(bf16[2,1024,128]{2,1,0:T(8,128)(2,1)} %fusion.46) | copy-start | bytes 1572868
  309.6 165.2 %all-reduce.3.cloned.1.call-start = ((), (), s32[]{:S(2)}) async-start(), calls=%async_computation.6 | async-start | bytes 4194304 | tf_op jit(solution)/shard_map/psum | solution.py:64
  323.2 10.7 %copy-start.5 = (bf16[2,1024,4,128]{1,3,2,0:T(8,128)(2,1)S(1)}, bf16[2,1024,4,128]{1,3,2,0:T(8,128)(2,1)}, u32[]{:S(2)}) copy-start(bf16[2,1024,4,128]{1,3,2,0:T(8,128)(2,1)} %copy.51) | copy-start | bytes 6291460
  333.9 21.2 %copy-start.12 = (f32[2048]{0:T(1024)S(1)}, f32[2048]{0:T(1024)}, u32[]{:S(2)}) copy-start(f32[2048]{0:T(1024)} %copy-done.11) | copy-start | bytes 24580
  333.9 21.2 %copy-start.16 = (f32[2,256]{1,0:T(2,128)S(1)}, f32[2,256]{1,0:T(2,128)}, u32[]{:S(2)}) copy-start(f32[2,256]{1,0:T(2,128)} %copy-done.15) | copy-start | bytes 6148
Sparse Core Ops, SparseCore 0:
  14.4 59.4 all-gather.2
  75.5 56.6 all-gather.4
  288.1 66.9 reduce-scatter.4
  357.5 66.9 reduce-scatter.2
  427.3 47.4 all-reduce.2
where the time goes:
time: 494 us; the launch traced here: 486 us
  matrix products  198 us (40%)
  waiting for transfers between devices  173 us (35%)
  other arithmetic  67.6 us (14%)
  local copies, waits for them, and re-layouts  26.6 us (5%)
  between operations  14.5 us (3%)
  blocking collectives  6.44 us (1%)
    reduce_scatter x1, waiting for transfers between devices, local_block(): lax.psum_scatter(out_part, 'tp', scatter_dimension=1, tiled=True)  59.1 us
    all_gather x1, waiting for transfers between devices, local_block(): act_full = lax.all_gather(act_local, 'tp', axis=1, tiled=True)  57.5 us
    psum x1, waiting for transfers between devices, local_block(): grad_w_key, grad_w_value = lax.psum((grad_w_key, grad_w_value), 'tp')  44.4 us
    convert_element_type x1, other arithmetic, local_block(): grad_scores = (attn_probs * (grad_probs - row_dot)).astype(jnp.bfloat16)  27.9 us
    dot_general x1, matrix products, local_block(): jnp.einsum('crie,cle->cirl', grad_att, value_proj, preferred_element_type...  24.8 us
    sub x1, matrix products, local_block(): attn_probs = jax.nn.softmax(jnp.where(causal, scores, -1e+30), axis=-1)  19.3 us
    dot_general x1, matrix products, local_block(): jnp.einsum('bse,de->bsd', grad_value, w_value, preferred_element_type=jnp...  15.5 us
    unnamed x52, local copies, waits for them, and re-layouts  15.2 us
  transfers between devices with their start and end apart: 5, of which 5 were waited for; matrix products, arithmetic and copies ran while one was open for 25% of the time, Pallas kernels for 0%

commit v1 on v0

v1 whole, which is shorter than its diff:
```python
import jax
import jax.numpy as jnp
from jax import lax
from jax.experimental import pallas as pl
from jax.experimental.pallas import tpu as pltpu
from jax.sharding import PartitionSpec as P

F32 = jnp.float32
BF16 = jnp.bfloat16
MESH = pl.DeviceIdType.MESH

TB = 256
NB = 2
TOK = TB * NB
SEQ = 1024
D = 2048
HD = 128
HL = 4
HW = HD * HL
SCALE = HD ** -0.5

W_SIB, W_X, W_Y, W_Z, W_YZ = 0, 1, 2, 3, 4
W_REL = 5
KV_SIB, KV_X, KV_REL = 9, 10, 11
BULK_X = 12
BULK_SIB = 16
BULK_REL = 20
RS_SIB, RS_SIB2, RS_X = 24, 25, 26
DKV_SIB, DKV_X, DKV_REL = 27, 28, 29
DW_SIB, DW_X, DW_XS = 30, 31, 32
OQ_SIB = 33
N_SEM = 34


def dot_nn(a, b):
    return jnp.dot(a, b, preferred_element_type=F32)


def dot_nt(a, b):
    return lax.dot_general(a, b, (((1,), (1,)), ((), ())), preferred_element_type=F32)


def dot_tn(a, b):
    return lax.dot_general(a, b, (((0,), (0,)), ((), ())), preferred_element_type=F32)


def rope(u, cos_t, sin_t):
    return u * cos_t + pltpu.roll(u, HD // 2, 1) * sin_t


def rope_back(u, cos_t, sin_t):
    return u * cos_t - pltpu.roll(u, HD // 2, 1) * sin_t


def attend(n, q, do, k_ref, b, kt_ref):
    keys = n * TB
    k = k_ref[b, 0:keys, 0:HD]
    v = k_ref[b, 0:keys, HD:2 * HD]
    s = dot_nt(k, q)
    row = lax.broadcasted_iota(jnp.int32, (TB, TB), 0)
    col = lax.broadcasted_iota(jnp.int32, (TB, TB), 1)
    last = jnp.where(row <= col, s[keys - TB:], -1e30)
    s = last if n == 1 else jnp.concatenate([s[:keys - TB], last], axis=0)
    e = jnp.exp(s - jnp.max(s, axis=0, keepdims=True))
    p = e * (1.0 / jnp.sum(e, axis=0, keepdims=True))
    p_low = p.astype(BF16)
    dp = dot_nt(v, do)
    ds = (p * (dp - jnp.sum(p * dp, axis=0, keepdims=True))).astype(BF16)
    o = dot_nn(kt_ref[b, HD:2 * HD, 0:keys], p_low).T
    dq = dot_nn(kt_ref[b, 0:HD, 0:keys], ds).T
    return o, dq, p_low, ds


def transpose_kv(kv_ref, kt_ref):
    for b in range(NB):
        for j in range(4):
            kt_ref[b, :, j * TB:(j + 1) * TB] = kv_ref[b, j * TB:(j + 1) * TB, :].astype(F32).T.astype(BF16)


def main_kernel(x_ref, act_ref, dout_ref, w_own, wkv_ref, gain_ref, cos_ref, sin_ref,
                out_ref, dx_ref, dw_ref, w_all, act_all, dout_all, kv_ref, dkv_ref, oq_ref,
                wbuf, q_s, do_s, o_s, dq_s, out_acc, da_acc, kt_ref, dkv_acc, rs_a, rs_b, rs_c, dw_parts,
                send, recv, lsem):
    dp = lax.axis_index('dp')
    tp = lax.axis_index('tp')
    sib = (dp, tp ^ 1)
    xp = (dp, tp ^ 2)
    xs = (dp, tp ^ 3)
    yp = (dp ^ 1, tp)
    zp = (dp ^ 2, tp)
    yzp = (dp ^ 3, tp)

    def rc(i, src, dst, dev):
        return pltpu.make_async_remote_copy(src_ref=src, dst_ref=dst, send_sem=send.at[i], recv_sem=recv.at[i],
                                            device_id=dev, device_id_type=MESH)

    def quarter(j):
        return pl.ds(pl.multiple_of((dp ^ j) * 128, 128), 128)

    def rows(blk):
        return pl.ds(pl.multiple_of(blk * TB, TB), TB)

    barrier = pltpu.get_barrier_semaphore()
    for dev in (sib, xp, xs, yp, zp, yzp):
        pl.semaphore_signal(barrier, inc=1, device_id=dev, device_id_type=MESH)
    pl.semaphore_wait(barrier, 6)

    copies = {}

    def start(i, src, dst, dev):
        copies[i] = rc(i, src, dst, dev)
        copies[i].start()

    start(W_X, w_own.at[:, quarter(0), :], w_all.at[2, :, quarter(0), :], xp)
    start(W_SIB, w_own, w_all.at[1], sib)
    start(BULK_SIB, dout_ref, dout_all.at[1], sib)
    start(BULK_SIB + 1, act_ref, act_all.at[1], sib)
    own_a = pltpu.make_async_copy(act_ref, act_all.at[0], lsem.at[1])
    own_a.start()
    own_d = pltpu.make_async_copy(dout_ref, dout_all.at[0], lsem.at[2])
    own_d.start()

    kv = dot_nn(act_ref[...], wkv_ref[...])
    k_rot = rope(kv[:, 0:HD].astype(BF16).astype(F32), cos_ref[...], sin_ref[...]).astype(BF16)
    v_own = kv[:, HD:2 * HD].astype(BF16)
    for b in range(NB):
        kv_ref[b, rows(tp), 0:HD] = k_rot[b * TB:(b + 1) * TB]
        kv_ref[b, rows(tp), HD:2 * HD] = v_own[b * TB:(b + 1) * TB]
    start(KV_X, kv_ref.at[:, rows(tp), :], kv_ref.at[:, rows(tp), :], xp)
    start(KV_SIB, kv_ref.at[:, rows(tp), :], kv_ref.at[:, rows(tp), :], sib)

    out_acc[...] = jnp.zeros_like(out_acc)
    da_acc[...] = jnp.zeros_like(da_acc)
    dkv_acc[...] = jnp.zeros_like(dkv_acc)

    def project():
        def pair(j, carry):
            cols = pl.ds(pl.multiple_of(j * 2 * HD, 2 * HD), 2 * HD)
            q = dot_nt(act_ref[...], wbuf[0, cols, :]).astype(BF16).astype(F32)
            for h in range(2):
                piece = rope(q[:, h * HD:(h + 1) * HD], cos_ref[...], sin_ref[...]) * SCALE
                q_s[:, pl.ds(pl.multiple_of((2 * j + h) * HD, HD), HD)] = piece.astype(BF16)
            do_s[:, cols] = dot_nt(dout_ref[...], wbuf[1, cols, :]).astype(BF16)
            return carry
        lax.fori_loop(0, HL // 2, pair, 0)

    def attend_group():
        for n in range(1, 5):
            @pl.when(tp == n - 1)
            def _():
                def step(t, carry):
                    b = t // 2
                    r = pl.ds(pl.multiple_of(b * TB, TB), TB)
                    cos_t = cos_ref[r, :]
                    sin_t = sin_ref[r, :]
                    for j in range(2):
                        c = pl.ds(pl.multiple_of(((t % 2) * 2 + j) * HD, HD), HD)
                        q = q_s[r, c]
                        do = do_s[r, c]
                        o, dq, p_low, ds = attend(n, q, do, kv_ref, b, kt_ref)
                        o_s[r, c] = o.astype(BF16)
                        dq_s[r, c] = rope_back(dq * SCALE, cos_t, sin_t).astype(BF16)
                        dkv_acc[b, 0:n * TB, 0:HD] += dot_nn(ds, q)
                        dkv_acc[b, 0:n * TB, HD:2 * HD] += dot_nn(p_low, do)
                    return carry
                lax.fori_loop(0, 4, step, 0)

    def accumulate():
        def tile(j, carry):
            cols = pl.ds(pl.multiple_of(j * 512, 512), 512)
            out_acc[:, cols] += dot_nn(o_s[...], wbuf[1, :, cols])
            da_acc[:, cols] += dot_nn(dq_s[...], wbuf[0, :, cols])
            return carry
        lax.fori_loop(0, 4, tile, 0)

    def load_w(src):
        cp = pltpu.make_async_copy(src, wbuf, lsem.at[0])
        cp.start()
        cp.wait()

    def exchange_kv():
        copies[KV_X].wait_recv()
        start(KV_REL, kv_ref.at[:, rows(tp ^ 2), :], kv_ref.at[:, rows(tp ^ 2), :], sib)
        copies[KV_SIB].wait_recv()
        copies[KV_REL].wait_recv()
        transpose_kv(kv_ref, kt_ref)

    def spread_w():
        copies[W_X].wait_recv()
        mine = w_all.at[2, :, quarter(0), :]
        start(W_Y, mine, mine, yp)
        start(W_Z, mine, mine, zp)
        start(W_YZ, mine, mine, yzp)
        start(W_REL, mine, w_all.at[3, :, quarter(0), :], sib)
        for b in range(NB):
            r = pl.ds(b * TB, TB)
            start(BULK_X + 2 * b, dout_ref.at[r, :], dout_all.at[2, r, :], xp)
            start(BULK_X + 2 * b + 1, act_ref.at[r, :], act_all.at[2, r, :], xp)

    load_w(w_own)
    project()
    spread_w()
    exchange_kv()

    def group(i, carry):
        @pl.when(i == 1)
        def _():
            rc(W_SIB, w_own, w_all.at[1], sib).wait_recv()

        @pl.when(i == 2)
        def _():
            for j, w in ((1, W_Y), (2, W_Z), (3, W_YZ)):
                piece = w_all.at[2, :, quarter(j), :]
                rc(w, piece, piece, sib).wait_recv()
                rc(W_REL + j, piece, w_all.at[3, :, quarter(j), :], sib).start()

        @pl.when(i == 3)
        def _():
            for j in range(4):
                rc(W_REL + j, w_all.at[2, :, quarter(j), :], w_all.at[3, :, quarter(j), :], sib).wait_recv()

        @pl.when(i > 0)
        def _():
            load_w(w_all.at[i])
            project()

        attend_group()
        accumulate()

        @pl.when(i == 0)
        def _():
            oq_ref[0, 0] = o_s[...]
            oq_ref[0, 1] = dq_s[...]

        @pl.when(i == 1)
        def _():
            rs_c[0] = o_s[...]
            rs_c[1] = dq_s[...]
        return carry

    lax.fori_loop(0, 4, group, 0)
    start(OQ_SIB, rs_c, oq_ref.at[1], sib)

    start(RS_SIB, dkv_acc.at[:, rows(tp ^ 1), :], rs_a.at[0], sib)
    start(RS_SIB2, dkv_acc.at[:, rows(tp ^ 3), :], rs_a.at[1], sib)
    for r in range(8):
        cols = slice(r * 256, (r + 1) * 256)
        out_ref[:, cols] = (x_ref[:, cols].astype(F32) + out_acc[:, cols]).astype(BF16)
    copies[RS_SIB].wait_recv()
    copies[RS_SIB2].wait_recv()
    rs_b[0] = dkv_acc[:, rows(tp ^ 2), :] + rs_a[1]
    start(RS_X, rs_b.at[0], rs_b.at[1], xp)

    for c in range(4):
        copies[BULK_X + c].wait_recv()
        r = pl.ds((c // 2) * TB, TB)
        whole = act_all if c % 2 else dout_all
        start(BULK_REL + c, whole.at[2, r, :], whole.at[3, r, :], sib)

    copies[RS_X].wait_recv()
    total = dkv_acc[:, rows(tp), :] + rs_a[0] + rs_b[1]
    for b in range(NB):
        r = slice(b * TB, (b + 1) * TB)
        dkv_ref[b, rows(tp), 0:HD] = rope_back(total[b, :, 0:HD], cos_ref[r], sin_ref[r]).astype(BF16)
        dkv_ref[b, rows(tp), HD:2 * HD] = total[b, :, HD:2 * HD].astype(BF16)
    start(DKV_X, dkv_ref.at[:, rows(tp), :], dkv_ref.at[:, rows(tp), :], xp)
    start(DKV_SIB, dkv_ref.at[:, rows(tp), :], dkv_ref.at[:, rows(tp), :], sib)

    dw_parts[0] = jnp.zeros((8, D), F32)

    def dx_rows(j, carry):
        b = j // 2
        r = pl.ds(pl.multiple_of(j * 128, 128), 128)
        d_own = dkv_ref[b, pl.ds(pl.multiple_of(tp * TB + (j % 2) * 128, 128), 128), :]
        da = da_acc[r, :] + dot_nt(d_own, wkv_ref[...])
        xf = x_ref[r, :].astype(F32)
        inv = lax.rsqrt(jnp.mean(xf * xf, axis=-1, keepdims=True) + 1e-6)
        normed = xf * inv
        prod = da * normed
        dw_parts[0] += jnp.sum(prod.reshape(16, 8, D), axis=0)
        gain = gain_ref[...]
        corr = jnp.mean(prod * gain, axis=-1, keepdims=True)
        dx_ref[r, :] = (dout_ref[r, :].astype(F32) + inv * (da * gain - normed * corr)).astype(BF16)
        return carry

    lax.fori_loop(0, 4, dx_rows, 0)
    start(DW_SIB, dw_parts.at[0], dw_parts.at[1], sib)
    start(DW_X, dw_parts.at[0], dw_parts.at[2], xp)
    start(DW_XS, dw_parts.at[0], dw_parts.at[3], xs)

    copies[DKV_X].wait_recv()
    start(DKV_REL, dkv_ref.at[:, rows(tp ^ 2), :], dkv_ref.at[:, rows(tp ^ 2), :], sib)
    for i in (DW_SIB, DW_X, DW_XS):
        copies[i].wait_recv()
    parts = [dw_parts[jnp.bitwise_xor(tp, t)] for t in range(4)]
    dw_ref[...] = jnp.sum(parts[0] + parts[1] + parts[2] + parts[3], axis=0, keepdims=True)

    copies[DKV_SIB].wait_recv()
    copies[DKV_REL].wait_recv()
    copies[OQ_SIB].wait_recv()
    for i in (BULK_SIB, BULK_SIB + 1, BULK_REL, BULK_REL + 1, BULK_REL + 2, BULK_REL + 3):
        copies[i].wait_recv()
    own_a.wait()
    own_d.wait()
    for i in copies:
        copies[i].wait_send()
    for j in (1, 2, 3):
        rc(W_REL + j, w_all.at[2, :, quarter(j), :], w_all.at[3, :, quarter(j), :], sib).wait_send()


def grad_kernel(act_ref, dout_ref, w_ref, kv_ref, dkv_ref, oq_ref, cos_ref, sin_ref,
                dwq_ref, dwo_ref, dwkv_ref, q_s, do_s, o_s, dq_s, kt_ref, dwkv_s):
    i = pl.program_id(0)
    tp = lax.axis_index('tp')
    blk = tp ^ i
    own_rows = pl.ds(pl.multiple_of(blk * TB, TB), TB)

    @pl.when(i == 0)
    def _():
        transpose_kv(kv_ref, kt_ref)
        dwq_ref[...] = jnp.zeros_like(dwq_ref)
        dwo_ref[...] = jnp.zeros_like(dwo_ref)

    @pl.when(i < 2)
    def _():
        o_s[...] = oq_ref[jnp.minimum(i, 1), 0]
        dq_s[...] = oq_ref[jnp.minimum(i, 1), 1]

    @pl.when(i >= 2)
    def _():
        def pair(j, carry):
            cols = pl.ds(pl.multiple_of(j * 2 * HD, 2 * HD), 2 * HD)
            q = dot_nt(act_ref[0], w_ref[0, cols, :]).astype(BF16).astype(F32)
            for b in range(NB):
                r = slice(b * TB, (b + 1) * TB)
                for h in range(2):
                    piece = rope(q[r, h * HD:(h + 1) * HD], cos_ref[b, own_rows, :], sin_ref[b, own_rows, :]) * SCALE
                    q_s[r, pl.ds(pl.multiple_of((2 * j + h) * HD, HD), HD)] = piece.astype(BF16)
            do_s[:, cols] = dot_nt(dout_ref[0], w_ref[1, cols, :]).astype(BF16)
            return carry
        lax.fori_loop(0, HL // 2, pair, 0)
        for n in range(1, 5):
            @pl.when(blk == n - 1)
            def _():
                def step(t, carry):
                    b = t // 2
                    r = pl.ds(pl.multiple_of(b * TB, TB), TB)
                    for j in range(2):
                        c = pl.ds(pl.multiple_of(((t % 2) * 2 + j) * HD, HD), HD)
                        o, dq, _, _ = attend(n, q_s[r, c], do_s[r, c], kv_ref, b, kt_ref)
                        o_s[r, c] = o.astype(BF16)
                        dq = rope_back(dq * SCALE, cos_ref[b, own_rows, :], sin_ref[b, own_rows, :])
                        dq_s[r, c] = dq.astype(BF16)
                    return carry
                lax.fori_loop(0, 4, step, 0)

    ot = o_s[...].astype(F32).T.astype(BF16)
    dqt = dq_s[...].astype(F32).T.astype(BF16)
    dkvt = jnp.concatenate([dkv_ref[b, own_rows, :].astype(F32).T for b in range(NB)], axis=1).astype(BF16)

    def tile(j, carry):
        cols = pl.ds(pl.multiple_of(j * 512, 512), 512)
        a = act_ref[0, :, cols]
        dwo_ref[:, cols] += dot_nn(ot, dout_ref[0, :, cols])
        dwq_ref[:, cols] += dot_nn(dqt, a)
        kv_part = dot_nn(dkvt, a)

        @pl.when(i % 2 == 0)
        def _():
            dwkv_s[i // 2, :, cols] = kv_part

        @pl.when(i % 2 == 1)
        def _():
            dwkv_s[i // 2, :, cols] += kv_part
        return carry

    lax.fori_loop(0, 4, tile, 0)

    @pl.when(i == 3)
    def _():
        dwkv_ref[...] = dwkv_s[0] + dwkv_s[1]


def local_block(hidden, positions, norm_w, w_query, w_key, w_value, w_out, grad_out):
    tp = lax.axis_index('tp')
    x = hidden.reshape(TOK, D)
    dout = grad_out.reshape(TOK, D)
    xf = x.astype(F32)
    inv_rms = lax.rsqrt(jnp.mean(xf * xf, axis=-1, keepdims=True) + 1e-6)
    gain = (1.0 + norm_w)[None, :]
    act = (xf * inv_rms * gain).astype(BF16)
    w_own = jnp.stack([w_query.T, w_out])
    wkv = jnp.concatenate([w_key, w_value], axis=1)
    half = HD // 2
    inv_freq = 10000.0 ** (-2.0 * jnp.arange(half, dtype=F32) / HD)
    angle = positions.astype(F32)[..., None] * inv_freq
    cos_t, sin_t = jnp.cos(angle), jnp.sin(angle)
    cos_all = jnp.concatenate([cos_t, cos_t], axis=-1)
    sin_all = jnp.concatenate([-sin_t, sin_t], axis=-1)
    cos_own = lax.dynamic_slice_in_dim(cos_all, tp * TB, TB, axis=1).reshape(TOK, HD)
    sin_own = lax.dynamic_slice_in_dim(sin_all, tp * TB, TB, axis=1).reshape(TOK, HD)

    vmem = pl.BlockSpec(memory_space=pltpu.VMEM)
    anym = pl.BlockSpec(memory_space=pl.ANY)
    sds = jax.ShapeDtypeStruct
    out, dx, dw, _, act_all, dout_all, kv, dkv, oq = pl.pallas_call(
        main_kernel,
        out_shape=[sds((TOK, D), BF16), sds((TOK, D), BF16), sds((1, D), F32), sds((4, 2, HW, D), BF16),
                   sds((4, TOK, D), BF16), sds((4, TOK, D), BF16), sds((NB, SEQ, 2 * HD), BF16),
                   sds((NB, SEQ, 2 * HD), BF16), sds((2, 2, TOK, HW), BF16)],
        in_specs=[vmem, vmem, vmem, anym, vmem, vmem, vmem, vmem],
        out_specs=[vmem, vmem, vmem, anym, anym, anym, vmem, vmem, vmem],
        scratch_shapes=[
            pltpu.VMEM((2, HW, D), BF16),
            pltpu.VMEM((TOK, HW), BF16), pltpu.VMEM((TOK, HW), BF16),
            pltpu.VMEM((TOK, HW), BF16), pltpu.VMEM((TOK, HW), BF16),
            pltpu.VMEM((TOK, D), F32), pltpu.VMEM((TOK, D), F32),
            pltpu.VMEM((NB, 2 * HD, SEQ), BF16),
            pltpu.VMEM((NB, SEQ, 2 * HD), F32),
            pltpu.VMEM((2, NB, TB, 2 * HD), F32), pltpu.VMEM((2, NB, TB, 2 * HD), F32),
            pltpu.VMEM((2, TOK, HW), BF16),
            pltpu.VMEM((4, 8, D), F32),
            pltpu.SemaphoreType.DMA((N_SEM,)), pltpu.SemaphoreType.DMA((N_SEM,)), pltpu.SemaphoreType.DMA((3,)),
        ],
        compiler_params=pltpu.CompilerParams(collective_id=0, has_side_effects=True, vmem_limit_bytes=64_000_000),
        name='main',
    )(x, act, dout, w_own, wkv, gain, cos_own, sin_own)

    whole = lambda s: pl.BlockSpec(s, lambda t: (0,) * len(s))
    chunk = pl.BlockSpec((1, TOK, D), lambda t: (t, 0, 0))
    dwq, dwo, dwkv = pl.pallas_call(
        grad_kernel,
        grid=(4,),
        out_shape=[sds((HW, D), F32), sds((HW, D), F32), sds((2 * HD, D), F32)],
        in_specs=[chunk, chunk, whole((2, HW, D)), whole((NB, SEQ, 2 * HD)), whole((NB, SEQ, 2 * HD)),
                  whole((2, 2, TOK, HW)), whole((NB, SEQ, HD)), whole((NB, SEQ, HD))],
        out_specs=[whole((HW, D)), whole((HW, D)), whole((2 * HD, D))],
        scratch_shapes=[pltpu.VMEM((TOK, HW), BF16)] * 4 + [pltpu.VMEM((NB, 2 * HD, SEQ), BF16), pltpu.VMEM((2, 2 * HD, D), F32)],
        compiler_params=pltpu.CompilerParams(vmem_limit_bytes=64_000_000),
        name='grads',
    )(act_all, dout_all, w_own, kv, dkv, oq, cos_all, sin_all)

    return (out.reshape(NB, TB, D), dx.reshape(NB, TB, D), dwq.T, dwo, dwkv[:HD].T, dwkv[HD:].T, dw.reshape(D))


def solution(mesh):
    specs_in = (P('dp', 'tp', None), P('dp', None), P(None), P(None, 'tp'), P(None, None), P(None, None), P('tp', None), P('dp', 'tp', None))
    specs_out = (P('dp', 'tp', None), P('dp', 'tp', None), P('dp', 'tp'), P(('dp', 'tp'), None), P('dp', None), P('dp', None), P('dp'))
    return jax.shard_map(local_block, mesh=mesh, in_specs=specs_in, out_specs=specs_out, check_vma=False)
```

time: 494 us -> 235 us (0.48); the launches traced: 486 us -> 235 us
  Pallas kernels: 0 us -> 201 us
  matrix products: 198 us -> 0 us
  waiting for transfers between devices: 173 us -> 0 us
  other arithmetic: 67.6 us -> 15.9 us
  between operations: 14.5 us -> 0.78 us
  local copies, waits for them, and re-layouts: 26.6 us -> 17.5 us
  blocking collectives: 6.44 us -> 0 us
    pallas_call x0 -> x2, Pallas kernels: none -> 201 us  [the longest x1 151 us: local_block(): pl.pallas_call(main_kernel, out_shape=[sds((TOK, D), BF16), sds((TOK, D),...]
    dot_general x17 -> x0, matrix products: 178 us -> none  [the longest x1 24.8 us: local_block(): jnp.einsum('crie,cle->cirl', grad_att, value_proj, preferred_element_type...]
    reduce_scatter x2 -> x0, waiting for transfers between devices: 70.3 us -> none  [the longest x1 59.1 us: local_block(): lax.psum_scatter(out_part, 'tp', scatter_dimension=1, tiled=True)]
    all_gather x2 -> x0, waiting for transfers between devices: 57.9 us -> none  [the longest x1 57.5 us: local_block(): act_full = lax.all_gather(act_local, 'tp', axis=1, tiled=True)]
    psum x1 -> x0, waiting for transfers between devices: 44.4 us -> none  [local_block(): grad_w_key, grad_w_value = lax.psum((grad_w_key, grad_w_value), 'tp')]
    convert_element_type x5 -> x2, other arithmetic: 39.9 us -> 1.88 us  [the longest x1 1.87 us: local_block(): act = (xf * inv_rms * gain).astype(BF16)]
    sub x1 -> x0, matrix products: 19.3 us -> none  [local_block(): attn_probs = jax.nn.softmax(jnp.where(causal, scores, -1e+30), axis=-1)]
    another operation x3 -> x1, other arithmetic: 12.1 us -> 3.99 us  [local_block(): w_own = jnp.stack([w_query.T, w_out])]
  transfers between devices with their start and end apart: 5 -> 0, of which waited for: 5 -> 0; matrix products, arithmetic and copies ran while one was open for 25% -> 0% of each run, Pallas kernels for 0% -> 0%
where the time goes in v1:
time: 235 us
  Pallas kernels  201 us (86%)
  local copies, waits for them, and re-layouts  17.5 us (7%)
  other arithmetic  15.9 us (7%)
    pallas_call x1, Pallas kernels, local_block(): pl.pallas_call(main_kernel, out_shape=[sds((TOK, D), BF16), sds((TOK, D),...  151 us
    pallas_call x1, Pallas kernels, local_block(): pl.pallas_call(grad_kernel, grid=(4,), out_shape=[sds((HW, D), F32), sds(...  49.5 us
    unnamed x26, local copies, waits for them, and re-layouts  15.8 us

profile of v1, /device:TPU:0, one launch (start us, length us, event | category | flops | bytes accessed | tf_op | source)
XLA Modules:
  0.0 234.9 jit_solution(15909123921477449702)
XLA Ops:
  0.6 0.0 copy-start.3
  0.6 0.0 copy-start.4
  0.7 0.0 copy-start.6
  0.7 0.0 copy-start.7
  0.7 0.0 copy-start
  0.7 2.2 multiply_reduce_fusion
  3.0 0.0 copy-done.6
  3.0 0.0 copy-start.5
  3.0 0.0 copy-done.7
  3.0 0.0 copy-done.3
  3.0 0.0 copy-done.4
  3.0 1.1 pad_maximum_fusion.1.wkv_ref
  4.1 0.0 copy-done
  4.1 1.9 multiply_convert_fusion.act_ref
  6.0 0.0 copy-done.5
  6.0 2.9 %copy.15 = bf16[2048,512]{0,1:T(8,128)(2,1)S(1)} copy(bf16[2048,512]{1,0:T(8,128)(2,1)} %param.11) | data formatting | bytes 4194304 | tf_op args[3]
  8.9 4.0 %pad_maximum_fusion.w_own.w_ref = bf16[2,512,2048]{2,1,0:T(8,128)(2,1)} fusion(bf16[1,512,2048]{2,1,0:T(8,128)(2,1)} %bitcast.27, bf16[1,512,2048]{2,1,0:T(8,128)(2,1)S(1)} %bitcast.22), kind=kLoop, calls=%fused_computation | loop fusion | flops 2097152 | bytes 8388608 | tf_op jit(solution)/shard_map/stack | solution.py:392
  12.9 3.7 %multiply_sine_fusion = (f32[2,1024,64]{2,1,0:T(8,128)S(1)}, f32[2,1024,64]{2,1,0:T(8,128)S(1)}, f32[2,1024,64]{2,1,0:T(8,128)S(1)}) fusion(f32[64]{0:T(128)S(1)} %multiply_power_fusion, f32[2,1024]{1,0:T(2,128)S(1)} %convert_element_type.15), kind=kLoop, calls=%fused_computation.3 | loop fusion | flops 262144 | bytes 1581312 | tf_op jit(solution)/shard_map/sin | solution.py:397
  16.6 1.0 fusion.1
  17.6 1.9 pad_maximum_fusion.2
  19.6 151.2 %main.1 = (bf16[512,2048]{1,0:T(8,128)(2,1)}, bf16[512,2048]{1,0:T(8,128)(2,1)}, f32[1,2048]{1,0:T(1,128)}, bf16[4,2,512,2048]{3,2,1,0:T(8,128)(2,1)}, bf16[4,51...) custom-call(bf16[512,2048]{1,0:T(8,128)(2,1)} %bitcast.21, ...), custom_call_target="tpu_custom_call" | custom-call | tf_op jit(solution)/shard_map/main/pallas_call | solution.py:406
  170.8 49.5 %grads.1 = (f32[512,2048]{1,0:T(8,128)}, f32[512,2048]{1,0:T(8,128)}, f32[256,2048]{1,0:T(8,128)}) custom-call(bf16[4,512,2048]{2,1,0:T(8,128)(2,1)} %get-tuple-element.20.act_ref, bf16[4,512,2048]{2,1,0:T(8,128)(2,1)} %get-tuple-element.21.dout_ref, bf16[2,512,2048]{2,1,0:T(8,128)(2,1)} %pad_maximum_fusion.w_own.w_ref, ...), custom_call_target="tpu_custom_call" | custom-call | tf_op jit(solution)/shard_map/grads/pallas_call | solution.py:431
  220.3 5.3 %copy.16 = f32[2048,512]{1,0:T(8,128)} copy(f32[2048,512]{0,1:T(8,128)} %bitcast.23) | data formatting | bytes 8388608
  225.6 1.7 slice_bitcast_fusion
  227.3 1.3 copy.18
  228.6 0.0 copy-start.2
  228.6 1.3 copy.17
  229.9 0.7 copy-done.2
  230.6 0.0 copy-start.1
  230.6 1.3 copy.23
  231.9 1.0 copy-done.1
  232.9 0.0 copy-start.8
  232.9 1.3 copy.24
  234.3 0.0 copy-done.8
  234.3 0.6 copy.25
  (5 shorter events, 0.0 us)
Async XLA Ops:
  0.6 2.4 %copy-start.3 = (bf16[2048,128]{1,0:T(8,128)(2,1)S(1)}, bf16[2048,128]{1,0:T(8,128)(2,1)}, u32[]{:S(2)}) copy-start(bf16[2048,128]{1,0:T(8,128)(2,1)} %param.13) | copy-start | bytes 1572868
  0.6 2.4 %copy-start.4 = (bf16[2048,128]{1,0:T(8,128)(2,1)S(1)}, bf16[2048,128]{1,0:T(8,128)(2,1)}, u32[]{:S(2)}) copy-start(bf16[2048,128]{1,0:T(8,128)(2,1)} %param.12) | copy-start | bytes 1572868
  0.7 2.3 copy-start.6
  0.7 2.3 copy-start.7
  0.7 3.4 %copy-start = (bf16[2,256,2048]{2,1,0:T(8,128)(2,1)S(1)}, bf16[2,256,2048]{2,1,0:T(8,128)(2,1)}, u32[]{:S(2)}) copy-start(bf16[2,256,2048]{2,1,0:T(8,128)(2,1)} %param.8) | copy-start | bytes 6291460
  3.0 3.0 %copy-start.5 = (f32[2048]{0:T(1024)}, f32[2048]{0:T(1024)S(1)}, u32[]{:S(2)}) copy-start(f32[2048]{0:T(1024)S(1)} %broadcast_add_fusion) | copy-start | bytes 24580
  228.6 2.0 copy-start.2
  230.6 2.3 copy-start.1
  232.9 1.3 copy-start.8

commit v2 on v0

v2 whole, which is shorter than its diff:
```python
import jax
import jax.numpy as jnp
from jax import lax
from jax.experimental import pallas as pl
from jax.experimental.pallas import tpu as pltpu
from jax.sharding import PartitionSpec as P

F32 = jnp.float32
BF16 = jnp.bfloat16
MESH = pl.DeviceIdType.MESH

TB = 256
NB = 2
TOK = TB * NB
SEQ = 1024
D = 2048
HD = 128
HL = 4
HW = HD * HL
SCALE = HD ** -0.5

WQ_X, WQ_Y, WQ_Z, WQ_YZ, WQ_REL, WQ_SIB = 0, 1, 2, 3, 4, 8
WO_X, WO_Y, WO_Z, WO_YZ, WO_REL, WO_SIB = 9, 10, 11, 12, 13, 17
KV_X, KV_SIB, KV_REL = 18, 19, 20
BULK_X, BULK_REL = 21, 25
DOUT_SIB, ACT_SIB = 29, 30
RS_SIB, RS_SIB2, RS_X = 31, 32, 33
DKV_X, DKV_SIB, DKV_REL = 35, 37, 39
DW_SIB, DW_X, DW_XS = 41, 42, 43
OQ_SIB = 44
N_SEM = 45


def dot_nn(a, b):
    return jnp.dot(a, b, preferred_element_type=F32)


def dot_nt(a, b):
    return lax.dot_general(a, b, (((1,), (1,)), ((), ())), preferred_element_type=F32)


def dot_tn(a, b):
    return lax.dot_general(a, b, (((0,), (0,)), ((), ())), preferred_element_type=F32)


def rope(u, cos_t, sin_t):
    return u * cos_t + pltpu.roll(u, HD // 2, 1) * sin_t


def rope_back(u, cos_t, sin_t):
    return u * cos_t - pltpu.roll(u, HD // 2, 1) * sin_t


def rope_back_t(u, cos_t, sin_t):
    swapped = jnp.concatenate([u[HD // 2:], u[:HD // 2]], axis=0)
    return u * cos_t - swapped * sin_t


def attend(n, q, do, k_ref, b, kt_ref):
    keys = n * TB
    k = k_ref[b, 0:keys, 0:HD]
    v = k_ref[b, 0:keys, HD:2 * HD]
    s = dot_nt(k, q)
    row = lax.broadcasted_iota(jnp.int32, (TB, TB), 0)
    col = lax.broadcasted_iota(jnp.int32, (TB, TB), 1)
    last = jnp.where(row <= col, s[keys - TB:], -1e30)
    s = last if n == 1 else jnp.concatenate([s[:keys - TB], last], axis=0)
    e = jnp.exp(s - jnp.max(s, axis=0, keepdims=True))
    p = e * (1.0 / jnp.sum(e, axis=0, keepdims=True))
    p_low = p.astype(BF16)
    dp = dot_nt(v, do)
    ds = (p * (dp - jnp.sum(p * dp, axis=0, keepdims=True))).astype(BF16)
    o_t = dot_nn(kt_ref[b, HD:2 * HD, 0:keys], p_low)
    dq_t = dot_nn(kt_ref[b, 0:HD, 0:keys], ds)
    return o_t, dq_t, p_low, ds


def transpose_kv(kv_ref, kt_ref):
    for b in range(NB):
        for j in range(4):
            kt_ref[b, :, j * TB:(j + 1) * TB] = kv_ref[b, j * TB:(j + 1) * TB, :].astype(F32).T.astype(BF16)


def main_kernel(x_hbm, dout_hbm, wq_own, wo_own, wk_own, wv_own, normw_ref, angle_hbm,
                out_hbm, dx_hbm, dw_ref, wq_all, wo_all, act_all, dout_all, dkv_hbm, oqt_hbm,
                x_ref, dout_ref, angle_ref, io_ref, dkv_ref, oqt, trig_t,
                act, kv_ref, wkv, cos_s, sin_s, wq_buf, wo_buf, q_s, do_s, o_s, dq_s, out_acc, da_acc, kt_ref,
                dkv_acc, rs_a, rs_b, rs_c, dw_parts, a_buf, d_buf, send, recv, lsem):
    dp = lax.axis_index('dp')
    tp = lax.axis_index('tp')
    sib = (dp, tp ^ 1)
    xp = (dp, tp ^ 2)
    xs = (dp, tp ^ 3)
    yp = (dp ^ 1, tp)
    zp = (dp ^ 2, tp)
    yzp = (dp ^ 3, tp)

    def rc(i, src, dst, dev):
        return pltpu.make_async_remote_copy(src_ref=src, dst_ref=dst, send_sem=send.at[i], recv_sem=recv.at[i],
                                            device_id=dev, device_id_type=MESH)

    def quarter(which, shard, j):
        size = 512 if which == 0 else 128
        r = pl.ds(pl.multiple_of((dp ^ j) * size, size), size)
        if shard is None:
            return (wq_own, wo_own)[which].at[r, :]
        return (wq_all, wo_all)[which].at[shard, r, :]

    def rows(blk):
        return pl.ds(pl.multiple_of(blk * TB, TB), TB)

    copies = {}

    def start(i, src, dst, dev):
        copies[i] = rc(i, src, dst, dev)
        copies[i].start()

    def local(i, src, dst):
        cp = pltpu.make_async_copy(src, dst, lsem.at[i])
        cp.start()
        return cp

    load_x = local(8, x_hbm, x_ref)
    load_a = local(9, angle_hbm, angle_ref)
    load_k = local(0, wk_own, wkv.at[:, 0:HD])
    load_v = local(1, wv_own, wkv.at[:, HD:2 * HD])
    load_q = local(2, wq_own, wq_buf.at[0])
    load_o = local(3, wo_own, wo_buf.at[0])
    load_d = local(4, dout_hbm, dout_ref)

    barrier = pltpu.get_barrier_semaphore()
    for dev in (sib, xp, xs, yp, zp, yzp):
        pl.semaphore_signal(barrier, inc=1, device_id=dev, device_id_type=MESH)
    pl.semaphore_wait(barrier, 6)

    start(WQ_X, quarter(0, None, 0), quarter(0, 2, 0), xp)
    start(WQ_SIB, wq_own, wq_all.at[1], sib)
    start(WO_SIB, wo_own, wo_all.at[1], sib)
    start(DOUT_SIB, dout_hbm, dout_all.at[1], sib)
    load_x.wait()
    load_a.wait()

    def norm_rows(j, carry):
        r = pl.ds(pl.multiple_of(j * 64, 64), 64)
        xf = x_ref[r, :].astype(F32)
        inv = lax.rsqrt(jnp.mean(xf * xf, axis=-1, keepdims=True) + 1e-6)
        act[r, :] = (xf * inv * (1.0 + normw_ref[...])).astype(BF16)
        return carry

    lax.fori_loop(0, TOK // 64, norm_rows, 0)
    lane = lax.broadcasted_iota(jnp.int32, (TB, HD), 1)

    def tables(blk):
        for b in range(NB):
            angle = angle_ref[b, rows(blk), :]
            sin_t = jnp.sin(angle)
            cos_s[b, rows(blk), :] = jnp.cos(angle)
            sin_s[b, rows(blk), :] = jnp.where(lane < HD // 2, -sin_t, sin_t)

    tables(tp)
    load_k.wait()
    load_v.wait()
    kv = dot_nn(act[...], wkv[...])
    for b in range(NB):
        r = slice(b * TB, (b + 1) * TB)
        k_rot = rope(kv[r, 0:HD].astype(BF16).astype(F32), cos_s[b, rows(tp), :], sin_s[b, rows(tp), :])
        kv_ref[b, rows(tp), 0:HD] = k_rot.astype(BF16)
        kv_ref[b, rows(tp), HD:2 * HD] = kv[r, HD:2 * HD].astype(BF16)
    own_kv = kv_ref.at[:, rows(tp), :]
    start(KV_X, own_kv, own_kv, xp)
    start(KV_SIB, own_kv, own_kv, sib)
    start(WO_X, quarter(1, None, 0), quarter(1, 2, 0), xp)
    start(BULK_X, dout_hbm.at[0:TB, :], dout_all.at[2, 0:TB, :], xp)
    start(ACT_SIB, act, act_all.at[1], sib)
    own_a = local(5, act, act_all.at[0])

    out_acc[...] = jnp.zeros_like(out_acc)
    da_acc[...] = jnp.zeros_like(da_acc)
    dkv_acc[...] = jnp.zeros_like(dkv_acc)

    def project(n_rows, a_src, d_src, slot, table):
        def pair(j, carry):
            cols = pl.ds(pl.multiple_of(j * 2 * HD, 2 * HD), 2 * HD)
            q = dot_nn(a_src[0:n_rows, :], wq_buf[slot, :, cols]).astype(BF16).astype(F32)
            for t in range(n_rows // TB):
                r = slice(t * TB, (t + 1) * TB)
                cos_t, sin_t = table(t)
                for h in range(2):
                    piece = rope(q[r, h * HD:(h + 1) * HD], cos_t, sin_t) * SCALE
                    q_s[r, pl.ds(pl.multiple_of((2 * j + h) * HD, HD), HD)] = piece.astype(BF16)
            do_s[0:n_rows, cols] = dot_nt(d_src[0:n_rows, :], wo_buf[slot, cols, :]).astype(BF16)
            return carry
        lax.fori_loop(0, HL // 2, pair, 0)

    def project_own(slot):
        project(TOK, act, dout_ref, slot, lambda b: (cos_s[b, rows(tp), :], sin_s[b, rows(tp), :]))

    def attend_group():
        for n in range(1, 5):
            @pl.when(tp == n - 1)
            def _():
                def step(t, carry):
                    b = t // 2
                    r = pl.ds(pl.multiple_of(b * TB, TB), TB)
                    cos_t = cos_s[b, rows(tp), :]
                    sin_t = sin_s[b, rows(tp), :]
                    for j in range(2):
                        c = pl.ds(pl.multiple_of(((t % 2) * 2 + j) * HD, HD), HD)
                        q = q_s[r, c]
                        do = do_s[r, c]
                        o_t, dq_t, p_low, ds = attend(n, q, do, kv_ref, b, kt_ref)
                        o_s[r, c] = o_t.T.astype(BF16)
                        dq_s[r, c] = rope_back(dq_t.T * SCALE, cos_t, sin_t).astype(BF16)
                        dkv_acc[b, 0:n * TB, 0:HD] += dot_nn(ds, q)
                        dkv_acc[b, 0:n * TB, HD:2 * HD] += dot_nn(p_low, do)
                    return carry
                lax.fori_loop(0, 4, step, 0)

    def accumulate(slot):
        def tile(j, carry):
            cols = pl.ds(pl.multiple_of(j * 512, 512), 512)
            out_acc[:, cols] += dot_nn(o_s[...], wo_buf[slot, :, cols])
            da_acc[:, cols] += dot_nt(dq_s[...], wq_buf[slot, cols, :])
            return carry
        lax.fori_loop(0, 4, tile, 0)

    def spread(which, ids):
        x_id, y_id, z_id, yz_id, rel_id = ids
        copies[x_id].wait_recv()
        mine = quarter(which, 2, 0)
        start(y_id, mine, mine, yp)
        start(z_id, mine, mine, zp)
        start(yz_id, mine, mine, yzp)
        start(rel_id, mine, quarter(which, 3, 0), sib)

    load_q.wait()
    load_o.wait()
    load_d.wait()
    own_d = local(4, dout_ref, dout_all.at[0])
    project_own(0)
    tables(tp ^ 2)
    tables(tp ^ 3)
    spread(0, (WQ_X, WQ_Y, WQ_Z, WQ_YZ, WQ_REL))
    copies[KV_X].wait_recv()
    other_kv = kv_ref.at[:, rows(tp ^ 2), :]
    start(KV_REL, other_kv, other_kv, sib)
    copies[KV_SIB].wait_recv()
    copies[KV_REL].wait_recv()
    transpose_kv(kv_ref, kt_ref)
    spread(1, (WO_X, WO_Y, WO_Z, WO_YZ, WO_REL))
    start(BULK_X + 1, act.at[0:TB, :], act_all.at[2, 0:TB, :], xp)
    start(BULK_X + 2, dout_hbm.at[TB:TOK, :], dout_all.at[2, TB:TOK, :], xp)
    start(BULK_X + 3, act.at[TB:TOK, :], act_all.at[2, TB:TOK, :], xp)

    def group(i, carry):
        slot = jnp.minimum(i, 1)

        @pl.when(i == 1)
        def _():
            rc(WQ_SIB, wq_own, wq_all.at[1], sib).wait_recv()
            rc(WO_SIB, wo_own, wo_all.at[1], sib).wait_recv()

        @pl.when(i == 2)
        def _():
            for which, first, rel in ((0, WQ_X, WQ_REL), (1, WO_X, WO_REL)):
                for j in (1, 2, 3):
                    piece = quarter(which, 2, j)
                    rc(first + j, piece, piece, sib).wait_recv()
                    rc(rel + j, piece, quarter(which, 3, j), sib).start()

        @pl.when(i == 3)
        def _():
            for which, rel in ((0, WQ_REL), (1, WO_REL)):
                for j in range(4):
                    rc(rel + j, quarter(which, 2, j), quarter(which, 3, j), sib).wait_recv()

        @pl.when(i > 0)
        def _():
            lq = local(2, wq_all.at[i], wq_buf.at[1])
            lo = local(3, wo_all.at[i], wo_buf.at[1])
            lq.wait()
            lo.wait()
            project_own(1)

        attend_group()
        accumulate(slot)

        @pl.when(i < 2)
        def _():
            for b in range(NB):
                r = slice(b * TB, (b + 1) * TB)
                o_t = o_s[r, :].astype(F32).T.astype(BF16)
                dq_t = dq_s[r, :].astype(F32).T.astype(BF16)

                @pl.when(i == 0)
                def _():
                    oqt[0, :, r] = o_t
                    oqt[1, :, r] = dq_t

                @pl.when(i == 1)
                def _():
                    rs_c[0, :, r] = o_t
                    rs_c[1, :, r] = dq_t
        return carry

    lax.fori_loop(0, 4, group, 0)

    start(RS_SIB, dkv_acc.at[:, rows(tp ^ 1), :], rs_a.at[0], sib)
    start(RS_SIB2, dkv_acc.at[:, rows(tp ^ 3), :], rs_a.at[1], sib)
    start(OQ_SIB, rs_c, oqt.at[:, :, TOK:2 * TOK], sib)
    for r in range(8):
        cols = slice(r * 256, (r + 1) * 256)
        io_ref[:, cols] = (x_ref[:, cols].astype(F32) + out_acc[:, cols]).astype(BF16)
    put_out = local(8, io_ref, out_hbm)
    copies[RS_SIB].wait_recv()
    copies[RS_SIB2].wait_recv()
    rs_b[0] = dkv_acc[:, rows(tp ^ 2), :] + rs_a[1]
    for b in range(NB):
        start(RS_X + b, rs_b.at[0, b], rs_b.at[1, b], xp)

    def head_part(t, carry):
        b = t // 2
        i = 2 + t % 2
        blk = tp ^ i
        r = pl.ds(pl.multiple_of(b * TB, TB), TB)

        def relay(c, whole):
            return rc(BULK_REL + 2 * b + c, whole.at[2, r, :], whole.at[3, r, :], sib)

        @pl.when(i == 2)
        def _():
            for c, whole in ((0, dout_all), (1, act_all)):
                rc(BULK_X + 2 * b + c, whole.at[2, r, :], whole.at[2, r, :], xp).wait_recv()
                relay(c, whole).start()

        @pl.when(i == 3)
        def _():
            relay(0, dout_all).wait_recv()
            relay(1, act_all).wait_recv()

        la = local(6, act_all.at[i, r, :], a_buf)
        ld = local(7, dout_all.at[i, r, :], d_buf)
        cos_t = cos_s.at[b, rows(blk), :]
        sin_t = sin_s.at[b, rows(blk), :]
        trig_t[0] = cos_t[...].T
        trig_t[1] = sin_t[...].T
        la.wait()
        ld.wait()
        project(TB, a_buf, d_buf, 0, lambda _: (cos_t[...], sin_t[...]))
        place = pl.ds(pl.multiple_of(i * TOK + b * TB, TB), TB)
        for n in range(1, 5):
            @pl.when(blk == n - 1)
            def _():
                def step(u, carry):
                    for j in range(2):
                        c = pl.ds(pl.multiple_of((u * 2 + j) * HD, HD), HD)
                        o_t, dq_t, _, _ = attend(n, q_s[0:TB, c], do_s[0:TB, c], kv_ref, b, kt_ref)
                        oqt[0, c, place] = o_t.astype(BF16)
                        oqt[1, c, place] = rope_back_t(dq_t * SCALE, trig_t[0], trig_t[1]).astype(BF16)
                    return carry
                lax.fori_loop(0, 2, step, 0)
        return carry

    lax.fori_loop(0, 4, head_part, 0)
    copies[OQ_SIB].wait_recv()
    put_oqt = local(9, oqt, oqt_hbm)
    put_out.wait()

    dw_parts[0] = jnp.zeros((8, D), F32)
    gain = 1.0 + normw_ref[...]

    def finish(b, carry):
        mine = pl.ds(pl.multiple_of(tp * TB, TB), TB)
        rc(RS_X + b, rs_b.at[0, b], rs_b.at[1, b], xp).wait_recv()
        total = dkv_acc[b, mine, :] + rs_a[0, b] + rs_b[1, b]
        dkv_ref[b, mine, 0:HD] = rope_back(total[:, 0:HD], cos_s[b, mine, :], sin_s[b, mine, :]).astype(BF16)
        dkv_ref[b, mine, HD:2 * HD] = total[:, HD:2 * HD].astype(BF16)
        piece = dkv_ref.at[b, mine, :]
        rc(DKV_X + b, piece, piece, xp).start()
        rc(DKV_SIB + b, piece, piece, sib).start()

        def dx_rows(j, carry):
            r = pl.ds(pl.multiple_of(b * TB + j * 128, 128), 128)
            d_own = dkv_ref[b, pl.ds(pl.multiple_of(tp * TB + j * 128, 128), 128), :]
            da = da_acc[r, :] + dot_nt(d_own, wkv[...])
            xf = x_ref[r, :].astype(F32)
            inv = lax.rsqrt(jnp.mean(xf * xf, axis=-1, keepdims=True) + 1e-6)
            normed = xf * inv
            prod = da * normed
            dw_parts[0] += jnp.sum(prod.reshape(16, 8, D), axis=0)
            corr = jnp.mean(prod * gain, axis=-1, keepdims=True)
            io_ref[r, :] = (dout_ref[r, :].astype(F32) + inv * (da * gain - normed * corr)).astype(BF16)
            return carry

        lax.fori_loop(0, 2, dx_rows, 0)
        return carry

    lax.fori_loop(0, NB, finish, 0)
    put_dx = local(8, io_ref, dx_hbm)
    start(DW_SIB, dw_parts.at[0], dw_parts.at[1], sib)
    start(DW_X, dw_parts.at[0], dw_parts.at[2], xp)
    start(DW_XS, dw_parts.at[0], dw_parts.at[3], xs)
    for b in range(NB):
        piece = dkv_ref.at[b, rows(tp ^ 2), :]
        rc(DKV_X + b, piece, piece, xp).wait_recv()
        start(DKV_REL + b, piece, piece, sib)
    for i in (DW_SIB, DW_X, DW_XS):
        copies[i].wait_recv()
    parts = [dw_parts[jnp.bitwise_xor(tp, t)] for t in range(4)]
    dw_ref[...] = jnp.sum(parts[0] + parts[1] + parts[2] + parts[3], axis=0, keepdims=True)

    for b in range(NB):
        piece = dkv_ref.at[b, rows(tp ^ 1), :]
        rc(DKV_SIB + b, piece, piece, sib).wait_recv()
        copies[DKV_REL + b].wait_recv()
    put_dkv = local(10, dkv_ref, dkv_hbm)
    copies[DOUT_SIB].wait_recv()
    copies[ACT_SIB].wait_recv()
    own_a.wait()
    own_d.wait()
    put_oqt.wait()
    put_dx.wait()
    put_dkv.wait()
    for i in copies:
        copies[i].wait_send()
    for which, rel in ((0, WQ_REL), (1, WO_REL)):
        for j in (1, 2, 3):
            rc(rel + j, quarter(which, 2, j), quarter(which, 3, j), sib).wait_send()
    for b in range(NB):
        piece = dkv_ref.at[b, rows(tp), :]
        rc(DKV_X + b, piece, piece, xp).wait_send()
        rc(DKV_SIB + b, piece, piece, sib).wait_send()
        r = slice(b * TB, (b + 1) * TB)
        rc(BULK_REL + 2 * b, dout_all.at[2, r, :], dout_all.at[3, r, :], sib).wait_send()
        rc(BULK_REL + 2 * b + 1, act_all.at[2, r, :], act_all.at[3, r, :], sib).wait_send()


def grad_kernel(act_ref, dout_ref, dkv_ref, oqt_ref, out_in, dx_in, dwq_ref, dwo_ref, dwk_ref, dwv_ref, out_ref, dx_ref, dkvt):
    tp = lax.axis_index('tp')
    out_ref[...] = out_in[...]
    dx_ref[...] = dx_in[...]

    @pl.when(pl.program_id(0) == 0)
    def _():
        for t in range(4):
            for b in range(NB):
                dkvt[t, :, b * TB:(b + 1) * TB] = dkv_ref[b, t * TB:(t + 1) * TB, :].astype(F32).T.astype(BF16)

    dwo_ref[...] = dot_nn(oqt_ref[0], dout_ref[...].reshape(4 * TOK, -1))
    dwq_ref[...] = dot_nn(oqt_ref[1], act_ref[...].reshape(4 * TOK, -1)).T
    total = dot_nn(dkvt[0], act_ref[jnp.bitwise_xor(tp, 0)])
    for t in range(1, 4):
        total += dot_nn(dkvt[t], act_ref[jnp.bitwise_xor(tp, t)])
    dwk_ref[...] = total[0:HD].T
    dwv_ref[...] = total[HD:2 * HD].T


def local_block(hidden, positions, norm_w, w_query, w_key, w_value, w_out, grad_out):
    x = hidden.reshape(TOK, D)
    dout = grad_out.reshape(TOK, D)
    half = HD // 2
    inv_freq = 10000.0 ** (-2.0 * (jnp.arange(HD) % half).astype(F32) / HD)
    angle = positions.astype(F32)[..., None] * inv_freq

    vmem = pl.BlockSpec(memory_space=pltpu.VMEM)
    anym = pl.BlockSpec(memory_space=pl.ANY)
    sds = jax.ShapeDtypeStruct
    out, dx, dw, _, _, act_all, dout_all, dkv, oqt = pl.pallas_call(
        main_kernel,
        out_shape=[sds((TOK, D), BF16), sds((TOK, D), BF16), sds((1, D), F32), sds((4, D, HW), BF16), sds((4, HW, D), BF16),
                   sds((4, TOK, D), BF16), sds((4, TOK, D), BF16), sds((NB, SEQ, 2 * HD), BF16), sds((2, HW, 4 * TOK), BF16)],
        in_specs=[anym, anym, anym, anym, anym, anym, vmem, anym],
        out_specs=[anym, anym, vmem, anym, anym, anym, anym, anym, anym],
        scratch_shapes=[
            pltpu.VMEM((TOK, D), BF16), pltpu.VMEM((TOK, D), BF16),
            pltpu.VMEM((NB, SEQ, HD), F32),
            pltpu.VMEM((TOK, D), BF16),
            pltpu.VMEM((NB, SEQ, 2 * HD), BF16),
            pltpu.VMEM((2, HW, 4 * TOK), BF16),
            pltpu.VMEM((2, HD, TB), F32),
            pltpu.VMEM((TOK, D), BF16),
            pltpu.VMEM((NB, SEQ, 2 * HD), BF16),
            pltpu.VMEM((D, 2 * HD), BF16),
            pltpu.VMEM((NB, SEQ, HD), F32), pltpu.VMEM((NB, SEQ, HD), F32),
            pltpu.VMEM((2, D, HW), BF16), pltpu.VMEM((2, HW, D), BF16),
            pltpu.VMEM((TOK, HW), BF16), pltpu.VMEM((TOK, HW), BF16),
            pltpu.VMEM((TOK, HW), BF16), pltpu.VMEM((TOK, HW), BF16),
            pltpu.VMEM((TOK, D), F32), pltpu.VMEM((TOK, D), F32),
            pltpu.VMEM((NB, 2 * HD, SEQ), BF16),
            pltpu.VMEM((NB, SEQ, 2 * HD), F32),
            pltpu.VMEM((2, NB, TB, 2 * HD), F32), pltpu.VMEM((2, NB, TB, 2 * HD), F32),
            pltpu.VMEM((2, TOK, HW), BF16),
            pltpu.VMEM((4, 8, D), F32),
            pltpu.VMEM((TB, D), BF16), pltpu.VMEM((TB, D), BF16),
            pltpu.SemaphoreType.DMA((N_SEM,)), pltpu.SemaphoreType.DMA((N_SEM,)), pltpu.SemaphoreType.DMA((11,)),
        ],
        compiler_params=pltpu.CompilerParams(collective_id=0, has_side_effects=True, vmem_limit_bytes=66_000_000),
        name='main',
    )(x, dout, w_query, w_out, w_key, w_value, norm_w[None, :], angle)

    whole = lambda s: pl.BlockSpec(s, lambda t: (0,) * len(s))
    cols = D // 8
    chunk = pl.BlockSpec((4, TOK, cols), lambda t: (0, 0, t))
    by_row = lambda r, c: pl.BlockSpec((r, c), lambda t: (t, 0))
    dwq, dwo, dwk, dwv, out, dx = pl.pallas_call(
        grad_kernel,
        grid=(8,),
        out_shape=[sds((D, HW), F32), sds((HW, D), F32), sds((D, HD), F32), sds((D, HD), F32), sds((TOK, D), BF16), sds((TOK, D), BF16)],
        in_specs=[chunk, chunk, whole((NB, SEQ, 2 * HD)), whole((2, HW, 4 * TOK)), by_row(TOK // 8, D), by_row(TOK // 8, D)],
        out_specs=[by_row(cols, HW), pl.BlockSpec((HW, cols), lambda t: (0, t)), by_row(cols, HD), by_row(cols, HD),
                   by_row(TOK // 8, D), by_row(TOK // 8, D)],
        scratch_shapes=[pltpu.VMEM((4, 2 * HD, TOK), BF16)],
        compiler_params=pltpu.CompilerParams(vmem_limit_bytes=64_000_000),
        name='grads',
    )(act_all, dout_all, dkv, oqt, out, dx)

    return out.reshape(NB, TB, D), dx.reshape(NB, TB, D), dwq, dwo, dwk, dwv, dw.reshape(D)


def solution(mesh):
    specs_in = (P('dp', 'tp', None), P('dp', None), P(None), P(None, 'tp'), P(None, None), P(None, None), P('tp', None), P('dp', 'tp', None))
    specs_out = (P('dp', 'tp', None), P('dp', 'tp', None), P('dp', 'tp'), P(('dp', 'tp'), None), P('dp', None), P('dp', None), P('dp'))
    return jax.shard_map(local_block, mesh=mesh, in_specs=specs_in, out_specs=specs_out, check_vma=False)
```

time: 494 us -> 173 us (0.35); the launches traced: 486 us -> 172 us
  matrix products: 198 us -> 0 us
  waiting for transfers between devices: 173 us -> 0 us
  Pallas kernels: 0 us -> 169 us
  other arithmetic: 67.6 us -> 2.02 us
  local copies, waits for them, and re-layouts: 26.6 us -> 0.61 us
  between operations: 14.5 us -> 0.67 us
  blocking collectives: 6.44 us -> 0 us
    dot_general x17 -> x0, matrix products: 178 us -> none  [the longest x1 24.8 us: local_block(): jnp.einsum('crie,cle->cirl', grad_att, value_proj, preferred_element_type...]
    pallas_call x0 -> x2, Pallas kernels: none -> 169 us  [the longest x1 149 us: local_block(): pl.pallas_call(main_kernel, out_shape=[sds((TOK, D), BF16), sds((TOK, D),...]
    reduce_scatter x2 -> x0, waiting for transfers between devices: 70.3 us -> none  [the longest x1 59.1 us: local_block(): lax.psum_scatter(out_part, 'tp', scatter_dimension=1, tiled=True)]
    all_gather x2 -> x0, waiting for transfers between devices: 57.9 us -> none  [the longest x1 57.5 us: local_block(): act_full = lax.all_gather(act_local, 'tp', axis=1, tiled=True)]
    psum x1 -> x0, waiting for transfers between devices: 44.4 us -> none  [local_block(): grad_w_key, grad_w_value = lax.psum((grad_w_key, grad_w_value), 'tp')]
    convert_element_type x5 -> x1, other arithmetic: 39.9 us -> 0.7 us  [local_block(): angle = positions.astype(F32)[..., None] * inv_freq]
    sub x1 -> x0, matrix products: 19.3 us -> none  [local_block(): attn_probs = jax.nn.softmax(jnp.where(causal, scores, -1e+30), axis=-1)]
    unnamed x52 -> x3, local copies, waits for them, and re-layouts: 15.2 us -> 0.61 us
  transfers between devices with their start and end apart: 5 -> 0, of which waited for: 5 -> 0; matrix products, arithmetic and copies ran while one was open for 25% -> 0% of each run, Pallas kernels for 0% -> 0%
where the time goes in v2:
time: 173 us; the launch traced here: 172 us
  Pallas kernels  169 us (98%)
  other arithmetic  2.02 us (1%)
    pallas_call x1, Pallas kernels, local_block(): pl.pallas_call(main_kernel, out_shape=[sds((TOK, D), BF16), sds((TOK, D),...  149 us
    pallas_call x1, Pallas kernels, local_block(): pl.pallas_call(grad_kernel, grid=(8,), out_shape=[sds((D, HW), F32), sds(...  20.4 us

profile of v2, /device:TPU:0, one launch (start us, length us, event | category | flops | bytes accessed | tf_op | source)
XLA Modules:
  0.0 172.4 jit_solution(14564882890426924328)
XLA Ops:
  0.6 0.7 convert_element_type.10
  1.3 1.3 broadcast_multiply_fusion.angle_hbm
  2.7 148.7 %main.1 = (bf16[512,2048]{1,0:T(8,128)(2,1)}, bf16[512,2048]{1,0:T(8,128)(2,1)}, f32[1,2048]{1,0:T(1,128)}, bf16[4,2048,512]{2,1,0:T(8,128)(2,1)}, bf16[4,512,20...) custom-call(bf16[512,2048]{1,0:T(8,128)(2,1)} %bitcast.6, ...), custom_call_target="tpu_custom_call" | custom-call | tf_op jit(solution)/shard_map/main/pallas_call | solution.py:468
  151.3 0.0 copy-start
  151.4 20.4 %grads.1 = (f32[2048,512]{1,0:T(8,128)}, f32[512,2048]{1,0:T(8,128)}, f32[2048,128]{1,0:T(8,128)}, f32[2048,128]{1,0:T(8,128)}, bf16[512,2048]{1,0:T(8,128)(2,1)}, /*index=5*/bf16[512,2048]{1,0:T(8,128)(2,1)}) custom-call(bf16[4,512,2048]{2,1,0:T(8,128)(2,1)} %get-tuple-element.20.act_ref, bf16[4,512,2048]{2,1,0:T(8,128)(2,1)} %get-tuple-element.21.dout_ref, ...), custom_call_target="tpu_custom_call" | custom-call | tf_op jit(solution)/shard_map/grads/pallas_call | solution.py:505
  171.8 0.0 copy-done
  171.8 0.6 copy.16
  (1 shorter events, 0.0 us)
Async XLA Ops:
  151.3 20.4 %copy-start = (f32[1,2048]{1,0:T(1,128)S(1)}, f32[1,2048]{1,0:T(1,128)}, u32[]{:S(2)}) copy-start(f32[1,2048]{1,0:T(1,128)} %get-tuple-element.32) | copy-start | bytes 24580

commit v3 on v2

v3 whole, which is shorter than its diff:
```python
import jax
import jax.numpy as jnp
import numpy as np
from jax import lax
from jax.experimental import pallas as pl
from jax.experimental.pallas import tpu as pltpu
from jax.sharding import PartitionSpec as P

F32 = jnp.float32
BF16 = jnp.bfloat16
MESH = pl.DeviceIdType.MESH

TB = 256
NB = 2
TOK = TB * NB
SEQ = 1024
D = 2048
HD = 128
HL = 4
HW = HD * HL
SCALE = HD ** -0.5

WQ_X, WQ_Y, WQ_Z, WQ_YZ, WQ_REL, WQ_SIB = 0, 1, 2, 3, 4, 8
WO_X, WO_Y, WO_Z, WO_YZ, WO_REL, WO_SIB = 9, 10, 11, 12, 13, 17
KV_X, KV_SIB, KV_REL = 18, 19, 20
BULK_X, BULK_REL = 21, 25
DOUT_SIB, ACT_SIB = 29, 30
RS_SIB, RS_SIB2, OQ_SIB = 31, 32, 33
DW_SIB, DW_X, DW_XS = 34, 35, 36
DKV_X, DKV_SIB, DKV_REL = 37, 41, 45
N_SEM = 49


def dot_nn(a, b):
    return jnp.dot(a, b, preferred_element_type=F32)


def dot_nt(a, b):
    return lax.dot_general(a, b, (((1,), (1,)), ((), ())), preferred_element_type=F32)


def dot_tn(a, b):
    return lax.dot_general(a, b, (((0,), (0,)), ((), ())), preferred_element_type=F32)


def rope(u, cos_t, sin_t):
    return u * cos_t + pltpu.roll(u, HD // 2, 1) * sin_t


def rope_back(u, cos_t, sin_t):
    return u * cos_t - pltpu.roll(u, HD // 2, 1) * sin_t


def rope_back_t(u, cos_t, sin_t):
    swapped = jnp.concatenate([u[HD // 2:], u[:HD // 2]], axis=0)
    return u * cos_t - swapped * sin_t


def attend(n, q, do, k_ref, b, kt_ref):
    keys = n * TB
    k = k_ref[b, 0:keys, 0:HD]
    v = k_ref[b, 0:keys, HD:2 * HD]
    s = dot_nt(k, q)
    row = lax.broadcasted_iota(jnp.int32, (TB, TB), 0)
    col = lax.broadcasted_iota(jnp.int32, (TB, TB), 1)
    last = jnp.where(row <= col, s[keys - TB:], -1e30)
    s = last if n == 1 else jnp.concatenate([s[:keys - TB], last], axis=0)
    e = jnp.exp(s - jnp.max(s, axis=0, keepdims=True))
    p = e * (1.0 / jnp.sum(e, axis=0, keepdims=True))
    p_low = p.astype(BF16)
    dp = dot_nt(v, do)
    ds = (p * (dp - jnp.sum(p * dp, axis=0, keepdims=True))).astype(BF16)
    o_t = dot_nn(kt_ref[b, HD:2 * HD, 0:keys], p_low)
    dq_t = dot_nn(kt_ref[b, 0:HD, 0:keys], ds)
    return o_t, dq_t, p_low, ds


def transpose_kv(kv_ref, kt_ref):
    for b in range(NB):
        for j in range(4):
            kt_ref[b, :, j * TB:(j + 1) * TB] = kv_ref[b, j * TB:(j + 1) * TB, :].astype(F32).T.astype(BF16)


def main_kernel(x_hbm, dout_hbm, wq_own, wo_own, wk_own, wv_own, normw_ref, pos_ref, freq_ref,
                out_hbm, dx_hbm, dw_ref, accq_hbm, acco_hbm, oqt_hbm, dkv_hbm, act_all, dout_all,
                x_ref, dout_ref, io_ref, dkv_ref, oqt, trig_t, dwq_acc,
                act, kv_ref, wkv, cos_s, sin_s, wq_buf, wo_buf, q_s, do_s, o_s, dq_s, out_acc, da_acc, kt_ref,
                dkv_acc, rs_a, rs_c, dw_parts, buf, send, recv, lsem):
    dp = lax.axis_index('dp')
    tp = lax.axis_index('tp')
    sib = (dp, tp ^ 1)
    xp = (dp, tp ^ 2)
    xs = (dp, tp ^ 3)
    yp = (dp ^ 1, tp)
    zp = (dp ^ 2, tp)
    yzp = (dp ^ 3, tp)

    def rc(i, src, dst, dev):
        return pltpu.make_async_remote_copy(src_ref=src, dst_ref=dst, send_sem=send.at[i], recv_sem=recv.at[i],
                                            device_id=dev, device_id_type=MESH)

    def quarter(which, shard, j):
        size = 512 if which == 0 else 128
        r = pl.ds(pl.multiple_of((dp ^ j) * size, size), size)
        if shard is None:
            return (wq_own, wo_own)[which].at[r, :]
        return (wq_buf, wo_buf)[which].at[shard, r, :]

    def rows(blk):
        return pl.ds(pl.multiple_of(blk * TB, TB), TB)

    copies = {}

    def start(i, src, dst, dev):
        copies[i] = rc(i, src, dst, dev)
        copies[i].start()

    def local(i, src, dst):
        cp = pltpu.make_async_copy(src, dst, lsem.at[i])
        cp.start()
        return cp

    def spread(which):
        first = (WQ_X, WO_X)[which]
        mine = quarter(which, 2, 0)
        rc(first, quarter(which, None, 0), mine, xp).wait_recv()
        for j, dev in ((1, yp), (2, zp), (3, yzp)):
            rc(first + j, mine, mine, dev).start()
        rc(first + 4, mine, quarter(which, 3, 0), sib).start()

    def bulk(c):
        r = pl.ds((c // 2) * TB, TB)
        src, dst = (act, act_all) if c % 2 else (dout_hbm, dout_all)
        return rc(BULK_X + c, src.at[r, :], dst.at[2, r, :], xp)

    load_x = local(8, x_hbm, x_ref)
    load_k = local(0, wk_own, wkv.at[:, 0:HD])
    load_v = local(1, wv_own, wkv.at[:, HD:2 * HD])
    load_q = local(2, wq_own, wq_buf.at[0])
    load_o = local(3, wo_own, wo_buf.at[0])
    load_d = local(4, dout_hbm, dout_ref)

    barrier = pltpu.get_barrier_semaphore()
    for dev in (sib, xp, xs, yp, zp, yzp):
        pl.semaphore_signal(barrier, inc=1, device_id=dev, device_id_type=MESH)
    pl.semaphore_wait(barrier, 6)

    start(WQ_X, quarter(0, None, 0), quarter(0, 2, 0), xp)
    start(WQ_SIB, wq_own, wq_buf.at[1], sib)
    start(WO_SIB, wo_own, wo_buf.at[1], sib)
    start(DOUT_SIB, dout_hbm, dout_all.at[1], sib)
    load_x.wait()

    def norm_rows(j, carry):
        r = pl.ds(pl.multiple_of(j * 64, 64), 64)
        xf = x_ref[r, :].astype(F32)
        inv = lax.rsqrt(jnp.mean(xf * xf, axis=-1, keepdims=True) + 1e-6)
        act[r, :] = (xf * inv * (1.0 + normw_ref[...])).astype(BF16)
        return carry

    lax.fori_loop(0, TOK // 64, norm_rows, 0)
    lane = lax.broadcasted_iota(jnp.int32, (HD, HD), 1)

    def tables(blk):
        for b in range(NB):
            for h in range(TB // HD):
                pos = pos_ref[b:b + 1, pl.ds(pl.multiple_of(blk * TB + h * HD, HD), HD)].astype(F32)
                angle = jnp.broadcast_to(pos, (HD, HD)).T * freq_ref[...]
                r = pl.ds(pl.multiple_of(blk * TB + h * HD, HD), HD)
                sin_t = jnp.sin(angle)
                cos_s[b, r, :] = jnp.cos(angle)
                sin_s[b, r, :] = jnp.where(lane < HD // 2, -sin_t, sin_t)

    tables(tp)
    load_k.wait()
    load_v.wait()
    kv = dot_nn(act[...], wkv[...])
    for b in range(NB):
        r = slice(b * TB, (b + 1) * TB)
        k_rot = rope(kv[r, 0:HD].astype(BF16).astype(F32), cos_s[b, rows(tp), :], sin_s[b, rows(tp), :])
        kv_ref[b, rows(tp), 0:HD] = k_rot.astype(BF16)
        kv_ref[b, rows(tp), HD:2 * HD] = kv[r, HD:2 * HD].astype(BF16)
    own_kv = kv_ref.at[:, rows(tp), :]
    start(KV_X, own_kv, own_kv, xp)
    start(KV_SIB, own_kv, own_kv, sib)
    start(WO_X, quarter(1, None, 0), quarter(1, 2, 0), xp)
    bulk(0).start()
    start(ACT_SIB, act, act_all.at[1], sib)
    own_a = local(5, act, act_all.at[0])

    out_acc[...] = jnp.zeros_like(out_acc)
    da_acc[...] = jnp.zeros_like(da_acc)
    dkv_acc[...] = jnp.zeros_like(dkv_acc)

    def project(n_rows, a_src, d_src, slot, table):
        def pair(j, carry):
            cols = pl.ds(pl.multiple_of(j * 2 * HD, 2 * HD), 2 * HD)
            q = dot_nn(a_src[0:n_rows, :], wq_buf[slot, :, cols]).astype(BF16).astype(F32)
            for t in range(n_rows // TB):
                r = slice(t * TB, (t + 1) * TB)
                cos_t, sin_t = table(t)
                for h in range(2):
                    piece = rope(q[r, h * HD:(h + 1) * HD], cos_t, sin_t) * SCALE
                    q_s[r, pl.ds(pl.multiple_of((2 * j + h) * HD, HD), HD)] = piece.astype(BF16)
            do_s[0:n_rows, cols] = dot_nt(d_src[0:n_rows, :], wo_buf[slot, cols, :]).astype(BF16)
            return carry
        lax.fori_loop(0, HL // 2, pair, 0)

    def project_own(slot):
        project(TOK, act, dout_ref, slot, lambda b: (cos_s[b, rows(tp), :], sin_s[b, rows(tp), :]))

    def attend_group():
        for n in range(1, 5):
            @pl.when(tp == n - 1)
            def _():
                def step(t, carry):
                    b = t // 2
                    r = pl.ds(pl.multiple_of(b * TB, TB), TB)
                    cos_t = cos_s[b, rows(tp), :]
                    sin_t = sin_s[b, rows(tp), :]
                    for j in range(2):
                        c = pl.ds(pl.multiple_of(((t % 2) * 2 + j) * HD, HD), HD)
                        q = q_s[r, c]
                        do = do_s[r, c]
                        o_t, dq_t, p_low, ds = attend(n, q, do, kv_ref, b, kt_ref)
                        o_s[r, c] = o_t.T.astype(BF16)
                        dq_s[r, c] = rope_back(dq_t.T * SCALE, cos_t, sin_t).astype(BF16)
                        dkv_acc[b, 0:n * TB, 0:HD] += dot_nn(ds, q)
                        dkv_acc[b, 0:n * TB, HD:2 * HD] += dot_nn(p_low, do)
                    return carry
                lax.fori_loop(0, 4, step, 0)

    def accumulate(slot):
        def tile(j, carry):
            cols = pl.ds(pl.multiple_of(j * 512, 512), 512)
            out_acc[:, cols] += dot_nn(o_s[...], wo_buf[slot, :, cols])
            da_acc[:, cols] += dot_nt(dq_s[...], wq_buf[slot, cols, :])
            return carry
        lax.fori_loop(0, 4, tile, 0)

    load_q.wait()
    load_o.wait()
    load_d.wait()
    own_d = local(4, dout_ref, dout_all.at[0])
    project_own(0)
    tables(tp ^ 2)
    tables(tp ^ 3)
    spread(0)
    copies[KV_X].wait_recv()
    other_kv = kv_ref.at[:, rows(tp ^ 2), :]
    start(KV_REL, other_kv, other_kv, sib)
    copies[KV_SIB].wait_recv()
    copies[KV_REL].wait_recv()
    transpose_kv(kv_ref, kt_ref)

    def group(i, carry):
        @pl.when(i == 1)
        def _():
            rc(WQ_SIB, wq_own, wq_buf.at[1], sib).wait_recv()
            rc(WO_SIB, wo_own, wo_buf.at[1], sib).wait_recv()

        @pl.when(i == 2)
        def _():
            for which, first in ((0, WQ_X), (1, WO_X)):
                for j in (1, 2, 3):
                    piece = quarter(which, 2, j)
                    rc(first + j, piece, piece, sib).wait_recv()
                    rc(first + 4 + j, piece, quarter(which, 3, j), sib).start()

        @pl.when(i == 3)
        def _():
            for which, rel in ((0, WQ_REL), (1, WO_REL)):
                for j in range(4):
                    rc(rel + j, quarter(which, 2, j), quarter(which, 3, j), sib).wait_recv()

        @pl.when(i > 0)
        def _():
            project_own(i)

        attend_group()

        @pl.when(i == 0)
        def _():
            spread(1)
            for c in (1, 2, 3):
                bulk(c).start()

        accumulate(i)

        @pl.when(i == 0)
        def _():
            oqt[0, 0] = o_s[...].astype(F32).T.astype(BF16)
            oqt[0, 1] = dq_s[...].astype(F32).T.astype(BF16)

        @pl.when(i == 1)
        def _():
            rs_c[0] = o_s[...].astype(F32).T.astype(BF16)
            rs_c[1] = dq_s[...].astype(F32).T.astype(BF16)
            rc(OQ_SIB, rs_c, oqt.at[1], sib).start()
        return carry

    lax.fori_loop(0, 4, group, 0)

    start(RS_SIB, dkv_acc.at[:, rows(tp ^ 1), :], rs_a.at[0], sib)
    start(RS_SIB2, dkv_acc.at[:, rows(tp ^ 3), :], rs_a.at[1], sib)
    for r in range(8):
        cols = slice(r * 256, (r + 1) * 256)
        io_ref[:, cols] = (x_ref[:, cols].astype(F32) + out_acc[:, cols]).astype(BF16)
    put_out = local(8, io_ref, out_hbm)
    copies[RS_SIB].wait_recv()
    copies[RS_SIB2].wait_recv()

    def dkv_piece(part, b, blk):
        return dkv_ref.at[part, b, rows(blk), :]

    for b in range(NB):
        for part, blk in ((0, tp), (1, tp ^ 2)):
            total = dkv_acc[b, rows(blk), :] + rs_a[part, b]
            d_k = rope_back(total[:, 0:HD], cos_s[b, rows(blk), :], sin_s[b, rows(blk), :])
            dkv_ref[part, b, rows(blk), 0:HD] = d_k.astype(BF16)
            dkv_ref[part, b, rows(blk), HD:2 * HD] = total[:, HD:2 * HD].astype(BF16)
    for b in range(NB):
        for part, blk in ((0, tp), (1, tp ^ 2)):
            piece = dkv_piece(part, b, blk)
            start(DKV_X + 2 * part + b, piece, piece, xp)
            start(DKV_SIB + 2 * part + b, piece, piece, sib)

    def weight_grads(first, o_t, dq_t, a_src, d_src):
        def tile(j, carry):
            cols = pl.ds(pl.multiple_of(j * 512, 512), 512)
            o_part = dot_nn(o_t[...], d_src[:, cols])
            q_part = dot_nn(dq_t[...], a_src[:, cols])
            if first:
                out_acc[:, cols] = o_part
                dwq_acc[:, cols] = q_part
            else:
                out_acc[:, cols] += o_part
                dwq_acc[:, cols] += q_part
            return carry
        lax.fori_loop(0, 4, tile, 0)

    copies[ACT_SIB].wait_recv()
    copies[DOUT_SIB].wait_recv()
    la = local(6, act_all.at[1], buf.at[0])
    ld = local(7, dout_all.at[1], buf.at[1])
    weight_grads(True, oqt.at[0, 0], oqt.at[0, 1], act, dout_ref)
    la.wait()
    ld.wait()
    rc(OQ_SIB, rs_c, oqt.at[1], sib).wait_recv()
    weight_grads(False, oqt.at[1, 0], oqt.at[1, 1], buf.at[0], buf.at[1])

    def head_part(t, carry):
        b = t // 2
        i = 2 + t % 2
        blk = tp ^ i
        r = pl.ds(pl.multiple_of(b * TB, TB), TB)

        def relay(c, whole):
            return rc(BULK_REL + 2 * b + c, whole.at[2, r, :], whole.at[3, r, :], sib)

        def load(k):
            half = pl.ds(k * TB, TB)
            return (pltpu.make_async_copy(act_all.at[2 + k, r, :], buf.at[0, half, :], lsem.at[6]),
                    pltpu.make_async_copy(dout_all.at[2 + k, r, :], buf.at[1, half, :], lsem.at[7]))

        @pl.when(i == 2)
        def _():
            for c, whole in ((0, dout_all), (1, act_all)):
                rc(BULK_X + 2 * b + c, whole.at[2, r, :], whole.at[2, r, :], xp).wait_recv()
                relay(c, whole).start()
            for cp in load(0):
                cp.start()

        cos_t = cos_s.at[b, rows(blk), :]
        sin_t = sin_s.at[b, rows(blk), :]
        trig_t[0] = cos_t[...].T
        trig_t[1] = sin_t[...].T
        half = pl.ds(pl.multiple_of((i - 2) * TB, TB), TB)
        for cp in load(0):
            cp.wait()
        project(TB, buf.at[0, half, :], buf.at[1, half, :], 0, lambda _: (cos_t[...], sin_t[...]))

        @pl.when(i == 2)
        def _():
            relay(0, dout_all).wait_recv()
            relay(1, act_all).wait_recv()
            for cp in load(1):
                cp.start()

        for n in range(1, 5):
            @pl.when(blk == n - 1)
            def _():
                def step(u, carry):
                    for j in range(2):
                        c = pl.ds(pl.multiple_of((u * 2 + j) * HD, HD), HD)
                        o_t, dq_t, _, _ = attend(n, q_s[0:TB, c], do_s[0:TB, c], kv_ref, b, kt_ref)
                        oqt[0, 0, c, half] = o_t.astype(BF16)
                        oqt[0, 1, c, half] = rope_back_t(dq_t * SCALE, trig_t[0], trig_t[1]).astype(BF16)
                    return carry
                lax.fori_loop(0, 2, step, 0)

        @pl.when(t == 1)
        def _():
            weight_grads(False, oqt.at[0, 0], oqt.at[0, 1], buf.at[0], buf.at[1])
            pltpu.make_async_copy(dwq_acc, accq_hbm, lsem.at[9]).start()
            pltpu.make_async_copy(out_acc, acco_hbm, lsem.at[10]).start()
        return carry

    lax.fori_loop(0, 4, head_part, 0)
    put_oqt = local(0, oqt.at[0], oqt_hbm)
    put_out.wait()

    dw_parts[0] = jnp.zeros((8, D), F32)
    gain = 1.0 + normw_ref[...]
    put_dkv = []

    for b in range(NB):
        for part, blk in ((0, tp ^ 2), (1, tp)):
            piece = dkv_piece(part, b, blk)
            rc(DKV_X + 2 * part + b, piece, piece, xp).wait_recv()
            start(DKV_REL + 2 * part + b, piece, piece, sib)

        def dx_rows(j, carry):
            r = pl.ds(pl.multiple_of(b * TB + j * 128, 128), 128)
            own = pl.ds(pl.multiple_of(tp * TB + j * 128, 128), 128)
            da = da_acc[r, :] + dot_nt(dkv_ref[0, b, own, :], wkv[...]) + dot_nt(dkv_ref[1, b, own, :], wkv[...])
            xf = x_ref[r, :].astype(F32)
            inv = lax.rsqrt(jnp.mean(xf * xf, axis=-1, keepdims=True) + 1e-6)
            normed = xf * inv
            prod = da * normed
            dw_parts[0] += jnp.sum(prod.reshape(16, 8, D), axis=0)
            corr = jnp.mean(prod * gain, axis=-1, keepdims=True)
            io_ref[r, :] = (dout_ref[r, :].astype(F32) + inv * (da * gain - normed * corr)).astype(BF16)
            return carry

        lax.fori_loop(0, 2, dx_rows, 0)
        if b == NB - 1:
            put_dx = local(8, io_ref, dx_hbm)
            start(DW_SIB, dw_parts.at[0], dw_parts.at[1], sib)
            start(DW_X, dw_parts.at[0], dw_parts.at[2], xp)
            start(DW_XS, dw_parts.at[0], dw_parts.at[3], xs)
        for part, blk, rel in ((0, tp ^ 1, tp ^ 3), (1, tp ^ 3, tp ^ 1)):
            piece = dkv_piece(part, b, blk)
            rc(DKV_SIB + 2 * part + b, piece, piece, sib).wait_recv()
            piece = dkv_piece(part, b, rel)
            rc(DKV_REL + 2 * part + b, piece, piece, sib).wait_recv()
        put_dkv.append(local(1 + b, dkv_ref.at[:, b], dkv_hbm.at[:, b]))

    for i in (DW_SIB, DW_X, DW_XS):
        copies[i].wait_recv()
    parts = [dw_parts[jnp.bitwise_xor(tp, t)] for t in range(4)]
    dw_ref[...] = jnp.sum(parts[0] + parts[1] + parts[2] + parts[3], axis=0, keepdims=True)

    own_a.wait()
    own_d.wait()
    for cp in (put_oqt, put_dx, *put_dkv):
        cp.wait()
    pltpu.make_async_copy(dwq_acc, accq_hbm, lsem.at[9]).wait()
    pltpu.make_async_copy(out_acc, acco_hbm, lsem.at[10]).wait()
    for i in copies:
        copies[i].wait_send()
    rc(OQ_SIB, rs_c, oqt.at[1], sib).wait_send()
    for c in range(4):
        bulk(c).wait_send()
        whole = act_all if c % 2 else dout_all
        r = slice((c // 2) * TB, (c // 2 + 1) * TB)
        rc(BULK_REL + c, whole.at[2, r, :], whole.at[3, r, :], sib).wait_send()
    for which, first in ((0, WQ_X), (1, WO_X)):
        for j in range(1, 8):
            rc(first + j, quarter(which, 2, j % 4), quarter(which, 2, j % 4), sib).wait_send()


def grad_kernel(accq_ref, acco_ref, act_ref, dout_ref, oqt_ref, dkv_ref, out_in, dx_in,
                dwq_ref, dwo_ref, dwk_ref, dwv_ref, out_ref, dx_ref, dkvt):
    tp = lax.axis_index('tp')
    out_ref[...] = out_in[...]
    dx_ref[...] = dx_in[...]

    @pl.when(pl.program_id(0) == 0)
    def _():
        for t in range(6):
            for b in range(NB):
                piece = dkv_ref[t // 4, b, (t % 4) * TB:(t % 4 + 1) * TB, :]
                dkvt[t, :, b * TB:(b + 1) * TB] = piece.astype(F32).T.astype(BF16)

    a = jnp.concatenate([act_ref[2, TB:TOK, :], act_ref[3, TB:TOK, :]], axis=0)
    d = dout_ref[...].reshape(TOK, -1)
    dwo_ref[...] = acco_ref[...] + dot_nn(oqt_ref[0], d)
    dwq_ref[...] = (accq_ref[...] + dot_nn(oqt_ref[1], a)).T
    total = dot_nn(dkvt[0], act_ref[jnp.bitwise_xor(tp, 0)])
    for t in range(1, 6):
        total += dot_nn(dkvt[t], act_ref[jnp.bitwise_xor(tp, t % 4)])
    dwk_ref[...] = total[0:HD].T
    dwv_ref[...] = total[HD:2 * HD].T


def local_block(hidden, positions, norm_w, w_query, w_key, w_value, w_out, grad_out):
    x = hidden.reshape(TOK, D)
    dout = grad_out.reshape(TOK, D)
    freq = 10000.0 ** (-2.0 * (np.arange(HD) % (HD // 2)) / HD)

    vmem = pl.BlockSpec(memory_space=pltpu.VMEM)
    anym = pl.BlockSpec(memory_space=pl.ANY)
    sds = jax.ShapeDtypeStruct
    out, dx, dw, accq, acco, oqt, dkv, act_all, dout_all = pl.pallas_call(
        main_kernel,
        out_shape=[sds((TOK, D), BF16), sds((TOK, D), BF16), sds((1, D), F32), sds((HW, D), F32), sds((HW, D), F32),
                   sds((2, HW, TOK), BF16), sds((2, NB, SEQ, 2 * HD), BF16), sds((4, TOK, D), BF16), sds((4, TOK, D), BF16)],
        in_specs=[anym, anym, anym, anym, anym, anym, vmem, vmem, vmem],
        out_specs=[anym, anym, vmem, anym, anym, anym, anym, anym, anym],
        scratch_shapes=[
            pltpu.VMEM((TOK, D), BF16), pltpu.VMEM((TOK, D), BF16), pltpu.VMEM((TOK, D), BF16),
            pltpu.VMEM((2, NB, SEQ, 2 * HD), BF16),
            pltpu.VMEM((2, 2, HW, TOK), BF16),
            pltpu.VMEM((2, HD, TB), F32),
            pltpu.VMEM((HW, D), F32),
            pltpu.VMEM((TOK, D), BF16),
            pltpu.VMEM((NB, SEQ, 2 * HD), BF16),
            pltpu.VMEM((D, 2 * HD), BF16),
            pltpu.VMEM((NB, SEQ, HD), F32), pltpu.VMEM((NB, SEQ, HD), F32),
            pltpu.VMEM((4, D, HW), BF16), pltpu.VMEM((4, HW, D), BF16),
            pltpu.VMEM((TOK, HW), BF16), pltpu.VMEM((TOK, HW), BF16),
            pltpu.VMEM((TOK, HW), BF16), pltpu.VMEM((TOK, HW), BF16),
            pltpu.VMEM((TOK, D), F32), pltpu.VMEM((TOK, D), F32),
            pltpu.VMEM((NB, 2 * HD, SEQ), BF16),
            pltpu.VMEM((NB, SEQ, 2 * HD), F32),
            pltpu.VMEM((2, NB, TB, 2 * HD), F32),
            pltpu.VMEM((2, HW, TOK), BF16),
            pltpu.VMEM((4, 8, D), F32),
            pltpu.VMEM((2, TOK, D), BF16),
            pltpu.SemaphoreType.DMA((N_SEM,)), pltpu.SemaphoreType.DMA((N_SEM,)), pltpu.SemaphoreType.DMA((11,)),
        ],
        compiler_params=pltpu.CompilerParams(collective_id=0, has_side_effects=True, vmem_limit_bytes=67_000_000),
        name='main',
    )(x, dout, w_query, w_out, w_key, w_value, norm_w[None, :], positions, jnp.asarray(freq[None, :], F32))

    whole = lambda s: pl.BlockSpec(s, lambda t: (0,) * len(s))
    cols = D // 8
    by_row = lambda r, c: pl.BlockSpec((r, c), lambda t: (t, 0))
    by_col = pl.BlockSpec((HW, cols), lambda t: (0, t))
    dwq, dwo, dwk, dwv, out, dx = pl.pallas_call(
        grad_kernel,
        grid=(8,),
        out_shape=[sds((D, HW), F32), sds((HW, D), F32), sds((D, HD), F32), sds((D, HD), F32), sds((TOK, D), BF16), sds((TOK, D), BF16)],
        in_specs=[by_col, by_col, pl.BlockSpec((4, TOK, cols), lambda t: (0, 0, t)), pl.BlockSpec((2, TB, cols), lambda t: (1, 1, t)),
                  whole((2, HW, TOK)), whole((2, NB, SEQ, 2 * HD)), by_row(TOK // 8, D), by_row(TOK // 8, D)],
        out_specs=[by_row(cols, HW), by_col, by_row(cols, HD), by_row(cols, HD), by_row(TOK // 8, D), by_row(TOK // 8, D)],
        scratch_shapes=[pltpu.VMEM((6, 2 * HD, TOK), BF16)],
        compiler_params=pltpu.CompilerParams(vmem_limit_bytes=64_000_000),
        name='grads',
    )(accq, acco, act_all, dout_all, oqt, dkv, out, dx)

    return out.reshape(NB, TB, D), dx.reshape(NB, TB, D), dwq, dwo, dwk, dwv, dw.reshape(D)


def solution(mesh):
    specs_in = (P('dp', 'tp', None), P('dp', None), P(None), P(None, 'tp'), P(None, None), P(None, None), P('tp', None), P('dp', 'tp', None))
    specs_out = (P('dp', 'tp', None), P('dp', 'tp', None), P('dp', 'tp'), P(('dp', 'tp'), None), P('dp', None), P('dp', None), P('dp'))
    return jax.shard_map(local_block, mesh=mesh, in_specs=specs_in, out_specs=specs_out, check_vma=False)
```

time: 173 us -> 167 us (0.965)
  Pallas kernels: 169 us -> 165 us
  other arithmetic: 2.02 us -> 0 us
    pallas_call x1, Pallas kernels: 20.4 us -> 17.8 us  [local_block(): pl.pallas_call(grad_kernel, grid=(8,), out_shape=[sds((D, HW), F32), sds(...]
where the time goes in v3:
time: 167 us; the launch traced here: 166 us
  Pallas kernels  165 us (99%)
    pallas_call x1, Pallas kernels, local_block(): pl.pallas_call(main_kernel, out_shape=[sds((TOK, D), BF16), sds((TOK, D),...  147 us
    pallas_call x1, Pallas kernels, local_block(): pl.pallas_call(grad_kernel, grid=(8,), out_shape=[sds((D, HW), F32), sds(...  17.8 us

profile of v3, /device:TPU:0, one launch (start us, length us, event | category | flops | bytes accessed | tf_op | source)
XLA Modules:
  0.0 166.4 jit_solution(18147010644233286832)
XLA Ops:
  0.6 147.3 %main.1 = (bf16[512,2048]{1,0:T(8,128)(2,1)}, bf16[512,2048]{1,0:T(8,128)(2,1)}, f32[1,2048]{1,0:T(1,128)}, f32[512,2048]{1,0:T(8,128)}, f32[512,2048]{1,0:T(8,1...) custom-call(bf16[512,2048]{1,0:T(8,128)(2,1)} %bitcast.6, ...), custom_call_target="tpu_custom_call" | custom-call | tf_op jit(solution)/shard_map/main/pallas_call | solution.py:505
  148.0 0.0 copy-start
  148.0 17.8 %grads.1 = (f32[2048,512]{1,0:T(8,128)}, f32[512,2048]{1,0:T(8,128)}, f32[2048,128]{1,0:T(8,128)}, f32[2048,128]{1,0:T(8,128)}, bf16[512,2048]{1,0:T(8,128)(2,1)}, /*index=5*/bf16[512,2048]{1,0:T(8,128)(2,1)}) custom-call(f32[512,2048]{1,0:T(8,128)} %get-tuple-element.22.accq_ref, f32[512,2048]{1,0:T(8,128)} %get-tuple-element.23.acco_ref, ...), custom_call_target="tpu_custom_call" | custom-call | tf_op jit(solution)/shard_map/grads/pallas_call | solution.py:541
  165.8 0.0 copy-done
  165.8 0.6 copy.17
Async XLA Ops:
  148.0 17.8 %copy-start = (f32[1,2048]{1,0:T(1,128)S(1)}, f32[1,2048]{1,0:T(1,128)}, u32[]{:S(2)}) copy-start(f32[1,2048]{1,0:T(1,128)} %get-tuple-element.36) | copy-start | bytes 24580

commit v4 on v3

--- a/solution.py
+++ b/solution.py
@@ -20,15 +20,15 @@
 HW = HD * HL
 SCALE = HD ** -0.5
 
-WQ_X, WQ_Y, WQ_Z, WQ_YZ, WQ_REL, WQ_SIB = 0, 1, 2, 3, 4, 8
-WO_X, WO_Y, WO_Z, WO_YZ, WO_REL, WO_SIB = 9, 10, 11, 12, 13, 17
-KV_X, KV_SIB, KV_REL = 18, 19, 20
-BULK_X, BULK_REL = 21, 25
-DOUT_SIB, ACT_SIB = 29, 30
-RS_SIB, RS_SIB2, OQ_SIB = 31, 32, 33
-DW_SIB, DW_X, DW_XS = 34, 35, 36
-DKV_X, DKV_SIB, DKV_REL = 37, 41, 45
-N_SEM = 49
+N_SEM = 51
+(WQ_X, _, _, _, WQ_REL, _, _, _, WQ_SIB,
+ WO_X, _, _, _, WO_REL, _, _, _, WO_SIB,
+ KV_X, KV_SIB, KV_REL, KV_LATE, _,
+ BULK_X, _, _, _, BULK_REL, _, _, _,
+ DOUT_SIB, ACT_SIB, RS_SIB, RS_SIB2, OQ_SIB, DW_SIB, DW_X, DW_XS,
+ DKV_X, _, _, _, DKV_SIB, _, _, _, DKV_REL, _, _, _) = range(N_SEM)
+KEY = slice(HD)
+VAL = slice(HD, 2 * HD)
 
 
 def dot_nn(a, b):
@@ -58,8 +58,8 @@
 
 def attend(n, q, do, k_ref, b, kt_ref):
     keys = n * TB
-    k = k_ref[b, 0:keys, 0:HD]
-    v = k_ref[b, 0:keys, HD:2 * HD]
+    k = k_ref[b, 0:keys, KEY]
+    v = k_ref[b, 0:keys, VAL]
     s = dot_nt(k, q)
     row = lax.broadcasted_iota(jnp.int32, (TB, TB), 0)
     col = lax.broadcasted_iota(jnp.int32, (TB, TB), 1)
@@ -70,15 +70,15 @@
     p_low = p.astype(BF16)
     dp = dot_nt(v, do)
     ds = (p * (dp - jnp.sum(p * dp, axis=0, keepdims=True))).astype(BF16)
-    o_t = dot_nn(kt_ref[b, HD:2 * HD, 0:keys], p_low)
-    dq_t = dot_nn(kt_ref[b, 0:HD, 0:keys], ds)
+    o_t = dot_nn(kt_ref[b, VAL, 0:keys], p_low)
+    dq_t = dot_nn(kt_ref[b, KEY, 0:keys], ds)
     return o_t, dq_t, p_low, ds
 
 
-def transpose_kv(kv_ref, kt_ref):
-    for b in range(NB):
-        for j in range(4):
-            kt_ref[b, :, j * TB:(j + 1) * TB] = kv_ref[b, j * TB:(j + 1) * TB, :].astype(F32).T.astype(BF16)
+def transpose_kv(kv_ref, kt_ref, b, later):
+    for j in range(2):
+        r = pl.ds(pl.multiple_of((2 * later + j) * TB, TB), TB)
+        kt_ref[b, :, r] = kv_ref[b, r, :].astype(F32).T.astype(BF16)
 
 
 def main_kernel(x_hbm, dout_hbm, wq_own, wo_own, wk_own, wv_own, normw_ref, pos_ref, freq_ref,
@@ -134,8 +134,8 @@
         return rc(BULK_X + c, src.at[r, :], dst.at[2, r, :], xp)
 
     load_x = local(8, x_hbm, x_ref)
-    load_k = local(0, wk_own, wkv.at[:, 0:HD])
-    load_v = local(1, wv_own, wkv.at[:, HD:2 * HD])
+    load_k = local(0, wk_own, wkv.at[:, KEY])
+    load_v = local(1, wv_own, wkv.at[:, VAL])
     load_q = local(2, wq_own, wq_buf.at[0])
     load_o = local(3, wo_own, wo_buf.at[0])
     load_d = local(4, dout_hbm, dout_ref)
@@ -177,11 +177,15 @@
     kv = dot_nn(act[...], wkv[...])
     for b in range(NB):
         r = slice(b * TB, (b + 1) * TB)
-        k_rot = rope(kv[r, 0:HD].astype(BF16).astype(F32), cos_s[b, rows(tp), :], sin_s[b, rows(tp), :])
-        kv_ref[b, rows(tp), 0:HD] = k_rot.astype(BF16)
-        kv_ref[b, rows(tp), HD:2 * HD] = kv[r, HD:2 * HD].astype(BF16)
+        k_rot = rope(kv[r, KEY].astype(BF16).astype(F32), cos_s[b, rows(tp), :], sin_s[b, rows(tp), :])
+        kv_ref[b, rows(tp), KEY] = k_rot.astype(BF16)
+        kv_ref[b, rows(tp), VAL] = kv[r, VAL].astype(BF16)
     own_kv = kv_ref.at[:, rows(tp), :]
-    start(KV_X, own_kv, own_kv, xp)
+
+    @pl.when(tp < 2)
+    def _():
+        rc(KV_X, own_kv, own_kv, xp).start()
+
     start(KV_SIB, own_kv, own_kv, sib)
     start(WO_X, quarter(1, None, 0), quarter(1, 2, 0), xp)
     bulk(0).start()
@@ -225,8 +229,8 @@
                         o_t, dq_t, p_low, ds = attend(n, q, do, kv_ref, b, kt_ref)
                         o_s[r, c] = o_t.T.astype(BF16)
                         dq_s[r, c] = rope_back(dq_t.T * SCALE, cos_t, sin_t).astype(BF16)
-                        dkv_acc[b, 0:n * TB, 0:HD] += dot_nn(ds, q)
-                        dkv_acc[b, 0:n * TB, HD:2 * HD] += dot_nn(p_low, do)
+                        dkv_acc[b, 0:n * TB, KEY] += dot_nn(ds, q)
+                        dkv_acc[b, 0:n * TB, VAL] += dot_nn(p_low, do)
                     return carry
                 lax.fori_loop(0, 4, step, 0)
 
@@ -246,12 +250,23 @@
     tables(tp ^ 2)
     tables(tp ^ 3)
     spread(0)
-    copies[KV_X].wait_recv()
     other_kv = kv_ref.at[:, rows(tp ^ 2), :]
-    start(KV_REL, other_kv, other_kv, sib)
+
+    @pl.when(tp >= 2)
+    def _():
+        rc(KV_X, other_kv, other_kv, xp).wait_recv()
+        rc(KV_REL, other_kv, other_kv, sib).start()
+
     copies[KV_SIB].wait_recv()
-    copies[KV_REL].wait_recv()
-    transpose_kv(kv_ref, kt_ref)
+    for b in range(NB):
+        transpose_kv(kv_ref, kt_ref, b, tp // 2)
+
+    @pl.when(tp >= 2)
+    def _():
+        sib_kv = kv_ref.at[:, rows(tp ^ 3), :]
+        rc(KV_REL, sib_kv, sib_kv, sib).wait_recv()
+        for b in range(NB):
+            transpose_kv(kv_ref, kt_ref, b, False)
 
     def group(i, carry):
         @pl.when(i == 1)
@@ -313,17 +328,23 @@
     def dkv_piece(part, b, blk):
         return dkv_ref.at[part, b, rows(blk), :]
 
-    for b in range(NB):
-        for part, blk in ((0, tp), (1, tp ^ 2)):
+    def reduce_kv(part, blk):
+        for b in range(NB):
             total = dkv_acc[b, rows(blk), :] + rs_a[part, b]
-            d_k = rope_back(total[:, 0:HD], cos_s[b, rows(blk), :], sin_s[b, rows(blk), :])
-            dkv_ref[part, b, rows(blk), 0:HD] = d_k.astype(BF16)
-            dkv_ref[part, b, rows(blk), HD:2 * HD] = total[:, HD:2 * HD].astype(BF16)
-    for b in range(NB):
-        for part, blk in ((0, tp), (1, tp ^ 2)):
+            d_k = rope_back(total[:, KEY], cos_s[b, rows(blk), :], sin_s[b, rows(blk), :])
+            dkv_ref[part, b, rows(blk), KEY] = d_k.astype(BF16)
+            dkv_ref[part, b, rows(blk), VAL] = total[:, VAL].astype(BF16)
+        for b in range(NB):
             piece = dkv_piece(part, b, blk)
-            start(DKV_X + 2 * part + b, piece, piece, xp)
-            start(DKV_SIB + 2 * part + b, piece, piece, sib)
+            rc(DKV_X + 2 * part + b, piece, piece, xp).start()
+            rc(DKV_SIB + 2 * part + b, piece, piece, sib).start()
+
+    reduce_kv(0, tp)
+
+    @pl.when(tp >= 2)
+    def _():
+        reduce_kv(1, tp ^ 2)
+        dkv_ref[1, :, rows(tp), :] = jnp.zeros((NB, TB, 2 * HD), BF16)
 
     def weight_grads(first, o_t, dq_t, a_src, d_src):
         def tile(j, carry):
@@ -378,6 +399,18 @@
         half = pl.ds(pl.multiple_of((i - 2) * TB, TB), TB)
         for cp in load(0):
             cp.wait()
+
+        def late_kv(blk):
+            piece = kv_ref.at[b, rows(blk), :]
+            return rc(KV_LATE + b, piece, piece, sib)
+
+        @pl.when((i == 2) & (tp < 2))
+        def _():
+            kv = dot_nn(buf[0, 0:TB, :], wkv[...])
+            kv_ref[b, rows(blk), KEY] = rope(kv[:, KEY].astype(BF16).astype(F32), cos_t[...], sin_t[...]).astype(BF16)
+            kv_ref[b, rows(blk), VAL] = kv[:, VAL].astype(BF16)
+            late_kv(tp ^ 2).start()
+
         project(TB, buf.at[0, half, :], buf.at[1, half, :], 0, lambda _: (cos_t[...], sin_t[...]))
 
         @pl.when(i == 2)
@@ -386,6 +419,11 @@
             relay(1, act_all).wait_recv()
             for cp in load(1):
                 cp.start()
+
+        @pl.when((i == 2) & (tp < 2))
+        def _():
+            late_kv(tp ^ 3).wait_recv()
+            transpose_kv(kv_ref, kt_ref, b, True)
 
         for n in range(1, 5):
             @pl.when(blk == n - 1)
@@ -415,10 +453,16 @@
     put_dkv = []
 
     for b in range(NB):
-        for part, blk in ((0, tp ^ 2), (1, tp)):
+        def take(part, blk):
             piece = dkv_piece(part, b, blk)
             rc(DKV_X + 2 * part + b, piece, piece, xp).wait_recv()
-            start(DKV_REL + 2 * part + b, piece, piece, sib)
+            rc(DKV_REL + 2 * part + b, piece, piece, sib).start()
+
+        take(0, tp ^ 2)
+
+        @pl.when(tp < 2)
+        def _():
+            take(1, tp)
 
         def dx_rows(j, carry):
             r = pl.ds(pl.multiple_of(b * TB + j * 128, 128), 128)
@@ -439,17 +483,28 @@
             start(DW_SIB, dw_parts.at[0], dw_parts.at[1], sib)
             start(DW_X, dw_parts.at[0], dw_parts.at[2], xp)
             start(DW_XS, dw_parts.at[0], dw_parts.at[3], xs)
-        for part, blk, rel in ((0, tp ^ 1, tp ^ 3), (1, tp ^ 3, tp ^ 1)):
+        def arrived(first, part, blk):
             piece = dkv_piece(part, b, blk)
-            rc(DKV_SIB + 2 * part + b, piece, piece, sib).wait_recv()
-            piece = dkv_piece(part, b, rel)
-            rc(DKV_REL + 2 * part + b, piece, piece, sib).wait_recv()
-        put_dkv.append(local(1 + b, dkv_ref.at[:, b], dkv_hbm.at[:, b]))
+            rc(first + 2 * part + b, piece, piece, sib).wait_recv()
+
+        arrived(DKV_SIB, 0, tp ^ 1)
+        arrived(DKV_REL, 0, tp ^ 3)
+
+        @pl.when(tp < 2)
+        def _():
+            arrived(DKV_REL, 1, tp ^ 1)
+
+        @pl.when(tp >= 2)
+        def _():
+            arrived(DKV_SIB, 1, tp ^ 3)
+
+        put_dkv.append(local(1 + b, dkv_ref.at[0, b], dkv_hbm.at[0, b]))
+        put_dkv.append(local(3 + b, dkv_ref.at[1, b, 0:TOK, :], dkv_hbm.at[1, b, 0:TOK, :]))
 
     for i in (DW_SIB, DW_X, DW_XS):
         copies[i].wait_recv()
     parts = [dw_parts[jnp.bitwise_xor(tp, t)] for t in range(4)]
-    dw_ref[...] = jnp.sum(parts[0] + parts[1] + parts[2] + parts[3], axis=0, keepdims=True)
+    dw_ref[...] = jnp.sum(sum(parts[1:], parts[0]), axis=0, keepdims=True)
 
     own_a.wait()
     own_d.wait()
@@ -460,6 +515,29 @@
     for i in copies:
         copies[i].wait_send()
     rc(OQ_SIB, rs_c, oqt.at[1], sib).wait_send()
+    for b in range(NB):
+        piece = dkv_piece(0, b, tp)
+        for i in (DKV_X, DKV_SIB, DKV_REL):
+            rc(i + b, piece, piece, sib).wait_send()
+
+        @pl.when(tp < 2)
+        def _():
+            rc(DKV_REL + 2 + b, piece, piece, sib).wait_send()
+            rc(KV_LATE + b, piece, piece, sib).wait_send()
+
+        @pl.when(tp >= 2)
+        def _():
+            rc(DKV_X + 2 + b, piece, piece, sib).wait_send()
+            rc(DKV_SIB + 2 + b, piece, piece, sib).wait_send()
+
+    @pl.when(tp < 2)
+    def _():
+        rc(KV_X, own_kv, own_kv, xp).wait_send()
+
+    @pl.when(tp >= 2)
+    def _():
+        rc(KV_REL, own_kv, own_kv, sib).wait_send()
+
     for c in range(4):
         bulk(c).wait_send()
         whole = act_all if c % 2 else dout_all
@@ -490,8 +568,8 @@
     total = dot_nn(dkvt[0], act_ref[jnp.bitwise_xor(tp, 0)])
     for t in range(1, 6):
         total += dot_nn(dkvt[t], act_ref[jnp.bitwise_xor(tp, t % 4)])
-    dwk_ref[...] = total[0:HD].T
-    dwv_ref[...] = total[HD:2 * HD].T
+    dwk_ref[...] = total[KEY].T
+    dwv_ref[...] = total[VAL].T
 
 
 def local_block(hidden, positions, norm_w, w_query, w_key, w_value, w_out, grad_out):
@@ -535,16 +613,17 @@
     )(x, dout, w_query, w_out, w_key, w_value, norm_w[None, :], positions, jnp.asarray(freq[None, :], F32))
 
     whole = lambda s: pl.BlockSpec(s, lambda t: (0,) * len(s))
-    cols = D // 8
+    steps = 4
+    cols = D // steps
     by_row = lambda r, c: pl.BlockSpec((r, c), lambda t: (t, 0))
     by_col = pl.BlockSpec((HW, cols), lambda t: (0, t))
     dwq, dwo, dwk, dwv, out, dx = pl.pallas_call(
         grad_kernel,
-        grid=(8,),
+        grid=(steps,),
         out_shape=[sds((D, HW), F32), sds((HW, D), F32), sds((D, HD), F32), sds((D, HD), F32), sds((TOK, D), BF16), sds((TOK, D), BF16)],
         in_specs=[by_col, by_col, pl.BlockSpec((4, TOK, cols), lambda t: (0, 0, t)), pl.BlockSpec((2, TB, cols), lambda t: (1, 1, t)),
-                  whole((2, HW, TOK)), whole((2, NB, SEQ, 2 * HD)), by_row(TOK // 8, D), by_row(TOK // 8, D)],
-        out_specs=[by_row(cols, HW), by_col, by_row(cols, HD), by_row(cols, HD), by_row(TOK // 8, D), by_row(TOK // 8, D)],
+                  whole((2, HW, TOK)), whole((2, NB, SEQ, 2 * HD)), by_row(TOK // steps, D), by_row(TOK // steps, D)],
+        out_specs=[by_row(cols, HW), by_col, by_row(cols, HD), by_row(cols, HD), by_row(TOK // steps, D), by_row(TOK // steps, D)],
         scratch_shapes=[pltpu.VMEM((6, 2 * HD, TOK), BF16)],
         compiler_params=pltpu.CompilerParams(vmem_limit_bytes=64_000_000),
         name='grads',
@@ -554,6 +633,6 @@
 
 
 def solution(mesh):
-    specs_in = (P('dp', 'tp', None), P('dp', None), P(None), P(None, 'tp'), P(None, None), P(None, None), P('tp', None), P('dp', 'tp', None))
-    specs_out = (P('dp', 'tp', None), P('dp', 'tp', None), P('dp', 'tp'), P(('dp', 'tp'), None), P('dp', None), P('dp', None), P('dp'))
+    specs_in = (P('dp', 'tp'), P('dp'), P(), P(None, 'tp'), P(), P(), P('tp'), P('dp', 'tp'))
+    specs_out = (P('dp', 'tp'), P('dp', 'tp'), P('dp', 'tp'), P(('dp', 'tp')), P('dp'), P('dp'), P('dp'))
     return jax.shard_map(local_block, mesh=mesh, in_specs=specs_in, out_specs=specs_out, check_vma=False)

time: 167 us -> 161 us (0.964)
  Pallas kernels: 165 us -> 160 us
    pallas_call x1, Pallas kernels: 147 us -> 144 us  [local_block(): pl.pallas_call(main_kernel, out_shape=[sds((TOK, D), BF16), sds((TOK, D),...]
    pallas_call x1, Pallas kernels: 17.8 us -> 15.6 us  [local_block(): pl.pallas_call(grad_kernel, grid=(steps,), out_shape=[sds((D, HW), F32),...]
where the time goes in v4:
time: 161 us
  Pallas kernels  160 us (99%)
    pallas_call x1, Pallas kernels, local_block(): pl.pallas_call(main_kernel, out_shape=[sds((TOK, D), BF16), sds((TOK, D),...  144 us
    pallas_call x1, Pallas kernels, local_block(): pl.pallas_call(grad_kernel, grid=(steps,), out_shape=[sds((D, HW), F32),...  15.6 us

profile of v4, /device:TPU:0, one launch (start us, length us, event | category | flops | bytes accessed | tf_op | source)
XLA Modules:
  0.0 161.2 jit_solution(16924640988160157969)
XLA Ops:
  0.6 144.3 %main.1 = (bf16[512,2048]{1,0:T(8,128)(2,1)}, bf16[512,2048]{1,0:T(8,128)(2,1)}, f32[1,2048]{1,0:T(1,128)}, f32[512,2048]{1,0:T(8,128)}, f32[512,2048]{1,0:T(8,1...) custom-call(bf16[512,2048]{1,0:T(8,128)(2,1)} %bitcast.6, ...), custom_call_target="tpu_custom_call" | custom-call | tf_op jit(solution)/shard_map/main/pallas_call | solution.py:583
  145.0 0.0 copy-start
  145.0 15.6 %grads.1 = (f32[2048,512]{1,0:T(8,128)}, f32[512,2048]{1,0:T(8,128)}, f32[2048,128]{1,0:T(8,128)}, f32[2048,128]{1,0:T(8,128)}, bf16[512,2048]{1,0:T(8,128)(2,1)}, /*index=5*/bf16[512,2048]{1,0:T(8,128)(2,1)}) custom-call(f32[512,2048]{1,0:T(8,128)} %get-tuple-element.22.accq_ref, f32[512,2048]{1,0:T(8,128)} %get-tuple-element.23.acco_ref, ...), custom_call_target="tpu_custom_call" | custom-call | tf_op jit(solution)/shard_map/grads/pallas_call | solution.py:620
  160.6 0.0 copy-done
  160.6 0.6 copy.17
Async XLA Ops:
  145.0 15.7 %copy-start = (f32[1,2048]{1,0:T(1,128)S(1)}, f32[1,2048]{1,0:T(1,128)}, u32[]{:S(2)}) copy-start(f32[1,2048]{1,0:T(1,128)} %get-tuple-element.36) | copy-start | bytes 24580

commit v5 on v4

--- a/solution.py
+++ b/solution.py
@@ -85,7 +85,7 @@
                 out_hbm, dx_hbm, dw_ref, accq_hbm, acco_hbm, oqt_hbm, dkv_hbm, act_all, dout_all,
                 x_ref, dout_ref, io_ref, dkv_ref, oqt, trig_t, dwq_acc,
                 act, kv_ref, wkv, cos_s, sin_s, wq_buf, wo_buf, q_s, do_s, o_s, dq_s, out_acc, da_acc, kt_ref,
-                dkv_acc, rs_a, rs_c, dw_parts, buf, send, recv, lsem):
+                dkv_acc, rs_a, rs_c, dw_acc, dw_parts, buf, send, recv, lsem):
     dp = lax.axis_index('dp')
     tp = lax.axis_index('tp')
     sib = (dp, tp ^ 1)
@@ -196,7 +196,7 @@
     da_acc[...] = jnp.zeros_like(da_acc)
     dkv_acc[...] = jnp.zeros_like(dkv_acc)
 
-    def project(n_rows, a_src, d_src, slot, table):
+    def project(n_rows, a_src, slot, table):
         def pair(j, carry):
             cols = pl.ds(pl.multiple_of(j * 2 * HD, 2 * HD), 2 * HD)
             q = dot_nn(a_src[0:n_rows, :], wq_buf[slot, :, cols]).astype(BF16).astype(F32)
@@ -206,12 +206,19 @@
                 for h in range(2):
                     piece = rope(q[r, h * HD:(h + 1) * HD], cos_t, sin_t) * SCALE
                     q_s[r, pl.ds(pl.multiple_of((2 * j + h) * HD, HD), HD)] = piece.astype(BF16)
-            do_s[0:n_rows, cols] = dot_nt(d_src[0:n_rows, :], wo_buf[slot, cols, :]).astype(BF16)
             return carry
         lax.fori_loop(0, HL // 2, pair, 0)
 
+    def project_back(d_src, slot, dst):
+        def pair(j, carry):
+            cols = pl.ds(pl.multiple_of(j * 2 * HD, 2 * HD), 2 * HD)
+            dst[:, cols] = dot_nt(d_src[...], wo_buf[slot, cols, :]).astype(BF16)
+            return carry
+        lax.fori_loop(0, HL // 2, pair, 0)
+
     def project_own(slot):
-        project(TOK, act, dout_ref, slot, lambda b: (cos_s[b, rows(tp), :], sin_s[b, rows(tp), :]))
+        project(TOK, act, slot, lambda b: (cos_s[b, rows(tp), :], sin_s[b, rows(tp), :]))
+        project_back(dout_ref, slot, do_s)
 
     def attend_group():
         for n in range(1, 5):
@@ -376,29 +383,40 @@
         blk = tp ^ i
         r = pl.ds(pl.multiple_of(b * TB, TB), TB)
 
-        def relay(c, whole):
-            return rc(BULK_REL + 2 * b + c, whole.at[2, r, :], whole.at[3, r, :], sib)
-
-        def load(k):
-            half = pl.ds(k * TB, TB)
-            return (pltpu.make_async_copy(act_all.at[2 + k, r, :], buf.at[0, half, :], lsem.at[6]),
-                    pltpu.make_async_copy(dout_all.at[2 + k, r, :], buf.at[1, half, :], lsem.at[7]))
+        def move(c, k):
+            whole = (dout_all, act_all)[c]
+            return (lambda: rc(BULK_X + 2 * b + c, whole.at[2, r, :], whole.at[2, r, :], xp),
+                    lambda: rc(BULK_REL + 2 * b + c, whole.at[2, r, :], whole.at[3, r, :], sib),
+                    lambda: pltpu.make_async_copy(whole.at[2 + k, r, :], buf.at[1 - c, pl.ds(k * TB, TB), :], lsem.at[7 - c]))
+
+        def receive(c):
+            over_x, relay, load = move(c, 0)
+            over_x().wait_recv()
+            relay().start()
+            load().start()
+
+        def receive_sibling(c):
+            _, relay, load = move(c, 1)
+            relay().wait_recv()
+            load().start()
+
+        half = pl.ds(pl.multiple_of((i - 2) * TB, TB), TB)
 
         @pl.when(i == 2)
         def _():
-            for c, whole in ((0, dout_all), (1, act_all)):
-                rc(BULK_X + 2 * b + c, whole.at[2, r, :], whole.at[2, r, :], xp).wait_recv()
-                relay(c, whole).start()
-            for cp in load(0):
-                cp.start()
+            receive(0)
+            move(0, 0)[-1]().wait()
+            receive_sibling(0)
+            project_back(buf.at[1, 0:TB, :], 0, do_s.at[0:TB, :])
+            move(0, 1)[-1]().wait()
+            project_back(buf.at[1, TB:TOK, :], 0, do_s.at[TB:TOK, :])
+            receive(1)
 
         cos_t = cos_s.at[b, rows(blk), :]
         sin_t = sin_s.at[b, rows(blk), :]
         trig_t[0] = cos_t[...].T
         trig_t[1] = sin_t[...].T
-        half = pl.ds(pl.multiple_of((i - 2) * TB, TB), TB)
-        for cp in load(0):
-            cp.wait()
+        move(1, 0)[-1]().wait()
 
         def late_kv(blk):
             piece = kv_ref.at[b, rows(blk), :]
@@ -411,14 +429,11 @@
             kv_ref[b, rows(blk), VAL] = kv[:, VAL].astype(BF16)
             late_kv(tp ^ 2).start()
 
-        project(TB, buf.at[0, half, :], buf.at[1, half, :], 0, lambda _: (cos_t[...], sin_t[...]))
+        project(TB, buf.at[0, half, :], 0, lambda _: (cos_t[...], sin_t[...]))
 
         @pl.when(i == 2)
         def _():
-            relay(0, dout_all).wait_recv()
-            relay(1, act_all).wait_recv()
-            for cp in load(1):
-                cp.start()
+            receive_sibling(1)
 
         @pl.when((i == 2) & (tp < 2))
         def _():
@@ -431,7 +446,7 @@
                 def step(u, carry):
                     for j in range(2):
                         c = pl.ds(pl.multiple_of((u * 2 + j) * HD, HD), HD)
-                        o_t, dq_t, _, _ = attend(n, q_s[0:TB, c], do_s[0:TB, c], kv_ref, b, kt_ref)
+                        o_t, dq_t, _, _ = attend(n, q_s[0:TB, c], do_s[half, c], kv_ref, b, kt_ref)
                         oqt[0, 0, c, half] = o_t.astype(BF16)
                         oqt[0, 1, c, half] = rope_back_t(dq_t * SCALE, trig_t[0], trig_t[1]).astype(BF16)
                     return carry
@@ -448,7 +463,7 @@
     put_oqt = local(0, oqt.at[0], oqt_hbm)
     put_out.wait()
 
-    dw_parts[0] = jnp.zeros((8, D), F32)
+    dw_acc[...] = jnp.zeros_like(dw_acc)
     gain = 1.0 + normw_ref[...]
     put_dkv = []
 
@@ -472,13 +487,14 @@
             inv = lax.rsqrt(jnp.mean(xf * xf, axis=-1, keepdims=True) + 1e-6)
             normed = xf * inv
             prod = da * normed
-            dw_parts[0] += jnp.sum(prod.reshape(16, 8, D), axis=0)
+            dw_acc[...] += jnp.sum(prod.reshape(-1, *dw_acc.shape), axis=0)
             corr = jnp.mean(prod * gain, axis=-1, keepdims=True)
             io_ref[r, :] = (dout_ref[r, :].astype(F32) + inv * (da * gain - normed * corr)).astype(BF16)
             return carry
 
         lax.fori_loop(0, 2, dx_rows, 0)
         if b == NB - 1:
+            dw_parts[0] = jnp.sum(dw_acc[...], axis=0, keepdims=True)
             put_dx = local(8, io_ref, dx_hbm)
             start(DW_SIB, dw_parts.at[0], dw_parts.at[1], sib)
             start(DW_X, dw_parts.at[0], dw_parts.at[2], xp)
@@ -504,7 +520,7 @@
     for i in (DW_SIB, DW_X, DW_XS):
         copies[i].wait_recv()
     parts = [dw_parts[jnp.bitwise_xor(tp, t)] for t in range(4)]
-    dw_ref[...] = jnp.sum(sum(parts[1:], parts[0]), axis=0, keepdims=True)
+    dw_ref[...] = sum(parts[1:], parts[0])
 
     own_a.wait()
     own_d.wait()
@@ -548,11 +564,12 @@
             rc(first + j, quarter(which, 2, j % 4), quarter(which, 2, j % 4), sib).wait_send()
 
 
-def grad_kernel(accq_ref, acco_ref, act_ref, dout_ref, oqt_ref, dkv_ref, out_in, dx_in,
-                dwq_ref, dwo_ref, dwk_ref, dwv_ref, out_ref, dx_ref, dkvt):
+def grad_kernel(accq_ref, acco_ref, act_ref, dout_ref, oqt_ref, dkv_ref, out_in, dx_in, dw_in,
+                dwq_ref, dwo_ref, dwk_ref, dwv_ref, out_ref, dx_ref, dw_ref, dkvt):
     tp = lax.axis_index('tp')
     out_ref[...] = out_in[...]
     dx_ref[...] = dx_in[...]
+    dw_ref[...] = dw_in[...]
 
     @pl.when(pl.program_id(0) == 0)
     def _():
@@ -604,7 +621,7 @@
             pltpu.VMEM((NB, SEQ, 2 * HD), F32),
             pltpu.VMEM((2, NB, TB, 2 * HD), F32),
             pltpu.VMEM((2, HW, TOK), BF16),
-            pltpu.VMEM((4, 8, D), F32),
+            pltpu.VMEM((8, D), F32), pltpu.VMEM((4, 1, D), F32),
             pltpu.VMEM((2, TOK, D), BF16),
             pltpu.SemaphoreType.DMA((N_SEM,)), pltpu.SemaphoreType.DMA((N_SEM,)), pltpu.SemaphoreType.DMA((11,)),
         ],
@@ -613,21 +630,21 @@
     )(x, dout, w_query, w_out, w_key, w_value, norm_w[None, :], positions, jnp.asarray(freq[None, :], F32))
 
     whole = lambda s: pl.BlockSpec(s, lambda t: (0,) * len(s))
-    steps = 4
+    steps = 2
     cols = D // steps
     by_row = lambda r, c: pl.BlockSpec((r, c), lambda t: (t, 0))
     by_col = pl.BlockSpec((HW, cols), lambda t: (0, t))
-    dwq, dwo, dwk, dwv, out, dx = pl.pallas_call(
+    dwq, dwo, dwk, dwv, out, dx, dw = pl.pallas_call(
         grad_kernel,
         grid=(steps,),
-        out_shape=[sds((D, HW), F32), sds((HW, D), F32), sds((D, HD), F32), sds((D, HD), F32), sds((TOK, D), BF16), sds((TOK, D), BF16)],
+        out_shape=[sds((D, HW), F32), sds((HW, D), F32), sds((D, HD), F32), sds((D, HD), F32), sds((TOK, D), BF16), sds((TOK, D), BF16), sds((1, D), F32)],
         in_specs=[by_col, by_col, pl.BlockSpec((4, TOK, cols), lambda t: (0, 0, t)), pl.BlockSpec((2, TB, cols), lambda t: (1, 1, t)),
-                  whole((2, HW, TOK)), whole((2, NB, SEQ, 2 * HD)), by_row(TOK // steps, D), by_row(TOK // steps, D)],
-        out_specs=[by_row(cols, HW), by_col, by_row(cols, HD), by_row(cols, HD), by_row(TOK // steps, D), by_row(TOK // steps, D)],
+                  whole((2, HW, TOK)), whole((2, NB, SEQ, 2 * HD)), by_row(TOK // steps, D), by_row(TOK // steps, D), whole((1, D))],
+        out_specs=[by_row(cols, HW), by_col, by_row(cols, HD), by_row(cols, HD), by_row(TOK // steps, D), by_row(TOK // steps, D), whole((1, D))],
         scratch_shapes=[pltpu.VMEM((6, 2 * HD, TOK), BF16)],
         compiler_params=pltpu.CompilerParams(vmem_limit_bytes=64_000_000),
         name='grads',
-    )(accq, acco, act_all, dout_all, oqt, dkv, out, dx)
+    )(accq, acco, act_all, dout_all, oqt, dkv, out, dx, dw)
 
     return out.reshape(NB, TB, D), dx.reshape(NB, TB, D), dwq, dwo, dwk, dwv, dw.reshape(D)
 

time: 161 us -> 158 us (0.981)
  Pallas kernels: 160 us -> 157 us
where the time goes in v5:
time: 158 us
  Pallas kernels  157 us (99%)
    pallas_call x1, Pallas kernels, local_block(): pl.pallas_call(main_kernel, out_shape=[sds((TOK, D), BF16), sds((TOK, D),...  143 us
    pallas_call x1, Pallas kernels, local_block(): pl.pallas_call(grad_kernel, grid=(steps,), out_shape=[sds((D, HW), F32),...  14.2 us

profile of v5, /device:TPU:0, one launch (start us, length us, event | category | flops | bytes accessed | tf_op | source)
XLA Modules:
  0.0 158.0 jit_solution(5181317869220129108)
XLA Ops:
  0.6 142.9 %main.1 = (bf16[512,2048]{1,0:T(8,128)(2,1)}, bf16[512,2048]{1,0:T(8,128)(2,1)}, f32[1,2048]{1,0:T(1,128)}, f32[512,2048]{1,0:T(8,128)}, f32[512,2048]{1,0:T(8,1...) custom-call(bf16[512,2048]{1,0:T(8,128)(2,1)} %bitcast.6, ...), custom_call_target="tpu_custom_call" | custom-call | tf_op jit(solution)/shard_map/main/pallas_call | solution.py:600
  143.5 14.2 %grads.1 = (f32[2048,512]{1,0:T(8,128)}, f32[512,2048]{1,0:T(8,128)}, f32[2048,128]{1,0:T(8,128)}, f32[2048,128]{1,0:T(8,128)}, bf16[512,2048]{1,0:T(8,128)(2,1)...) custom-call(f32[512,2048]{1,0:T(8,128)} %get-tuple-element.23.accq_ref, f32[512,2048]{1,0:T(8,128)} %get-tuple-element.24.acco_ref, ...), custom_call_target="tpu_custom_call" | custom-call | tf_op jit(solution)/shard_map/grads/pallas_call | solution.py:637

commit v6 on v5

--- a/solution.py
+++ b/solution.py
@@ -20,10 +20,10 @@
 HW = HD * HL
 SCALE = HD ** -0.5
 
-N_SEM = 51
+N_SEM = 52
 (WQ_X, _, _, _, WQ_REL, _, _, _, WQ_SIB,
  WO_X, _, _, _, WO_REL, _, _, _, WO_SIB,
- KV_X, KV_SIB, KV_REL, KV_LATE, _,
+ KV_X, KV_SIB, KV_REL, KV_LATE, _, BULK_END,
  BULK_X, _, _, _, BULK_REL, _, _, _,
  DOUT_SIB, ACT_SIB, RS_SIB, RS_SIB2, OQ_SIB, DW_SIB, DW_X, DW_XS,
  DKV_X, _, _, _, DKV_SIB, _, _, _, DKV_REL, _, _, _) = range(N_SEM)
@@ -115,6 +115,9 @@
         copies[i] = rc(i, src, dst, dev)
         copies[i].start()
 
+    def first_quarter(which, i):
+        start(i, quarter(which, None, 0), quarter(which, 2, 0), xp)
+
     def local(i, src, dst):
         cp = pltpu.make_async_copy(src, dst, lsem.at[i])
         cp.start()
@@ -129,9 +132,21 @@
         rc(first + 4, mine, quarter(which, 3, 0), sib).start()
 
     def bulk(c):
-        r = pl.ds((c // 2) * TB, TB)
+        r = pl.ds((c // 2) * TB, HD if c == 3 else TB)
         src, dst = (act, act_all) if c % 2 else (dout_hbm, dout_all)
         return rc(BULK_X + c, src.at[r, :], dst.at[2, r, :], xp)
+
+    def bulk_end():
+        r = pl.ds(TOK - HD, HD)
+        return rc(BULK_END, act.at[r, :], act_all.at[2, r, :], xp)
+
+    def receive(c):
+        whole = act_all if c % 2 else dout_all
+        r = pl.ds((c // 2) * TB, TB)
+        bulk(c).wait_recv()
+        if c == 3:
+            bulk_end().wait_recv()
+        rc(BULK_REL + c, whole.at[2, r, :], whole.at[3, r, :], sib).start()
 
     load_x = local(8, x_hbm, x_ref)
     load_k = local(0, wk_own, wkv.at[:, KEY])
@@ -145,7 +160,7 @@
         pl.semaphore_signal(barrier, inc=1, device_id=dev, device_id_type=MESH)
     pl.semaphore_wait(barrier, 6)
 
-    start(WQ_X, quarter(0, None, 0), quarter(0, 2, 0), xp)
+    first_quarter(0, WQ_X)
     start(WQ_SIB, wq_own, wq_buf.at[1], sib)
     start(WO_SIB, wo_own, wo_buf.at[1], sib)
     start(DOUT_SIB, dout_hbm, dout_all.at[1], sib)
@@ -187,7 +202,7 @@
         rc(KV_X, own_kv, own_kv, xp).start()
 
     start(KV_SIB, own_kv, own_kv, sib)
-    start(WO_X, quarter(1, None, 0), quarter(1, 2, 0), xp)
+    first_quarter(1, WO_X)
     bulk(0).start()
     start(ACT_SIB, act, act_all.at[1], sib)
     own_a = local(5, act, act_all.at[0])
@@ -198,7 +213,7 @@
 
     def project(n_rows, a_src, slot, table):
         def pair(j, carry):
-            cols = pl.ds(pl.multiple_of(j * 2 * HD, 2 * HD), 2 * HD)
+            cols = pl.ds(pl.multiple_of(j * TB, TB), TB)
             q = dot_nn(a_src[0:n_rows, :], wq_buf[slot, :, cols]).astype(BF16).astype(F32)
             for t in range(n_rows // TB):
                 r = slice(t * TB, (t + 1) * TB)
@@ -211,7 +226,7 @@
 
     def project_back(d_src, slot, dst):
         def pair(j, carry):
-            cols = pl.ds(pl.multiple_of(j * 2 * HD, 2 * HD), 2 * HD)
+            cols = pl.ds(pl.multiple_of(j * TB, TB), TB)
             dst[:, cols] = dot_nt(d_src[...], wo_buf[slot, cols, :]).astype(BF16)
             return carry
         lax.fori_loop(0, HL // 2, pair, 0)
@@ -243,7 +258,7 @@
 
     def accumulate(slot):
         def tile(j, carry):
-            cols = pl.ds(pl.multiple_of(j * 512, 512), 512)
+            cols = pl.ds(pl.multiple_of(j * HW, HW), HW)
             out_acc[:, cols] += dot_nn(o_s[...], wo_buf[slot, :, cols])
             da_acc[:, cols] += dot_nt(dq_s[...], wq_buf[slot, cols, :])
             return carry
@@ -275,6 +290,14 @@
         for b in range(NB):
             transpose_kv(kv_ref, kt_ref, b, False)
 
+    def weight_grad(acc, first, left, src):
+        def tile(j, carry):
+            cols = pl.ds(pl.multiple_of(j * HW, HW), HW)
+            part = dot_nn(left[...], src[:, cols])
+            acc[:, cols] = part if first else acc[:, cols] + part
+            return carry
+        lax.fori_loop(0, 4, tile, 0)
+
     def group(i, carry):
         @pl.when(i == 1)
         def _():
@@ -283,6 +306,12 @@
 
         @pl.when(i == 2)
         def _():
+            copies[ACT_SIB].wait_recv()
+            load = local(6, act_all.at[1], buf.at[0])
+            weight_grad(dwq_acc, True, oqt.at[0, 1], act)
+            load.wait()
+            rc(OQ_SIB, rs_c, oqt.at[1], sib).wait_recv()
+            weight_grad(dwq_acc, False, oqt.at[1, 1], buf.at[0])
             for which, first in ((0, WQ_X), (1, WO_X)):
                 for j in (1, 2, 3):
                     piece = quarter(which, 2, j)
@@ -322,6 +351,8 @@
         return carry
 
     lax.fori_loop(0, 4, group, 0)
+    copies[DOUT_SIB].wait_recv()
+    load_sib = local(7, dout_all.at[1], buf.at[1])
 
     start(RS_SIB, dkv_acc.at[:, rows(tp ^ 1), :], rs_a.at[0], sib)
     start(RS_SIB2, dkv_acc.at[:, rows(tp ^ 3), :], rs_a.at[1], sib)
@@ -346,36 +377,59 @@
             rc(DKV_X + 2 * part + b, piece, piece, xp).start()
             rc(DKV_SIB + 2 * part + b, piece, piece, sib).start()
 
-    reduce_kv(0, tp)
-
     @pl.when(tp >= 2)
     def _():
         reduce_kv(1, tp ^ 2)
         dkv_ref[1, :, rows(tp), :] = jnp.zeros((NB, TB, 2 * HD), BF16)
 
-    def weight_grads(first, o_t, dq_t, a_src, d_src):
-        def tile(j, carry):
-            cols = pl.ds(pl.multiple_of(j * 512, 512), 512)
-            o_part = dot_nn(o_t[...], d_src[:, cols])
-            q_part = dot_nn(dq_t[...], a_src[:, cols])
-            if first:
-                out_acc[:, cols] = o_part
-                dwq_acc[:, cols] = q_part
-            else:
-                out_acc[:, cols] += o_part
-                dwq_acc[:, cols] += q_part
+    bulk_end().start()
+    reduce_kv(0, tp)
+
+    for c in range(2):
+        receive(c)
+    weight_grad(out_acc, True, oqt.at[0, 0], dout_ref)
+    load_sib.wait()
+    weight_grad(out_acc, False, oqt.at[1, 0], buf.at[1])
+    own_a.wait()
+    own_d.wait()
+    put_out.wait()
+
+    def take(part, b, blk):
+        piece = dkv_piece(part, b, blk)
+        rc(DKV_X + NB * part + b, piece, piece, xp).wait_recv()
+        rc(DKV_REL + NB * part + b, piece, piece, sib).start()
+
+    def dw_copies():
+        return [rc(DW_SIB + k, dw_parts.at[0], dw_parts.at[k + 1], dev) for k, dev in enumerate((sib, xp, xs))]
+
+    def finish_dx():
+        @pl.when(tp < 2)
+        def _():
+            for b in range(NB):
+                take(1, b, tp)
+
+        dw_acc[...] = jnp.zeros_like(dw_acc)
+        gain = 1.0 + normw_ref[...]
+
+        def dx_rows(j, carry):
+            b = j // 2
+            r = pl.ds(pl.multiple_of(j * HD, HD), HD)
+            own = pl.ds(pl.multiple_of(tp * TB + (j % 2) * HD, HD), HD)
+            da = da_acc[r, :] + dot_nt(dkv_ref[0, b, own, :], wkv[...]) + dot_nt(dkv_ref[1, b, own, :], wkv[...])
+            xf = x_ref[r, :].astype(F32)
+            inv = lax.rsqrt(jnp.mean(xf * xf, axis=-1, keepdims=True) + 1e-6)
+            normed = xf * inv
+            prod = da * normed
+            dw_acc[...] += jnp.sum(prod.reshape(-1, *dw_acc.shape), axis=0)
+            corr = jnp.mean(prod * gain, axis=-1, keepdims=True)
+            io_ref[r, :] = (dout_ref[r, :].astype(F32) + inv * (da * gain - normed * corr)).astype(BF16)
             return carry
-        lax.fori_loop(0, 4, tile, 0)
-
-    copies[ACT_SIB].wait_recv()
-    copies[DOUT_SIB].wait_recv()
-    la = local(6, act_all.at[1], buf.at[0])
-    ld = local(7, dout_all.at[1], buf.at[1])
-    weight_grads(True, oqt.at[0, 0], oqt.at[0, 1], act, dout_ref)
-    la.wait()
-    ld.wait()
-    rc(OQ_SIB, rs_c, oqt.at[1], sib).wait_recv()
-    weight_grads(False, oqt.at[1, 0], oqt.at[1, 1], buf.at[0], buf.at[1])
+
+        lax.fori_loop(0, TOK // HD, dx_rows, 0)
+        dw_parts[0] = jnp.sum(dw_acc[...], axis=0, keepdims=True)
+        pltpu.make_async_copy(io_ref, dx_hbm, lsem.at[8]).start()
+        for cp in dw_copies():
+            cp.start()
 
     def head_part(t, carry):
         b = t // 2
@@ -383,40 +437,46 @@
         blk = tp ^ i
         r = pl.ds(pl.multiple_of(b * TB, TB), TB)
 
-        def move(c, k):
+        def load(c, k):
             whole = (dout_all, act_all)[c]
-            return (lambda: rc(BULK_X + 2 * b + c, whole.at[2, r, :], whole.at[2, r, :], xp),
-                    lambda: rc(BULK_REL + 2 * b + c, whole.at[2, r, :], whole.at[3, r, :], sib),
-                    lambda: pltpu.make_async_copy(whole.at[2 + k, r, :], buf.at[1 - c, pl.ds(k * TB, TB), :], lsem.at[7 - c]))
-
-        def receive(c):
-            over_x, relay, load = move(c, 0)
-            over_x().wait_recv()
-            relay().start()
-            load().start()
-
-        def receive_sibling(c):
-            _, relay, load = move(c, 1)
-            relay().wait_recv()
-            load().start()
+            return pltpu.make_async_copy(whole.at[2 + k, r, :], buf.at[1 - c, pl.ds(k * TB, TB), :], lsem.at[7 - c + 5 * k])
+
+        def load_relayed(c):
+            whole = (dout_all, act_all)[c]
+            rc(BULK_REL + 2 * b + c, whole.at[2, r, :], whole.at[3, r, :], sib).wait_recv()
+            load(c, 1).start()
 
         half = pl.ds(pl.multiple_of((i - 2) * TB, TB), TB)
 
         @pl.when(i == 2)
         def _():
-            receive(0)
-            move(0, 0)[-1]().wait()
-            receive_sibling(0)
-            project_back(buf.at[1, 0:TB, :], 0, do_s.at[0:TB, :])
-            move(0, 1)[-1]().wait()
-            project_back(buf.at[1, TB:TOK, :], 0, do_s.at[TB:TOK, :])
-            receive(1)
+            load(0, 0).start()
+            load_relayed(0)
+
+            @pl.when(b == 0)
+            def _():
+                load(1, 0).start()
+
+            for k in range(2):
+                load(0, k).wait()
+                part = slice(k * TB, (k + 1) * TB)
+                project_back(buf.at[1, part, :], 0, do_s.at[part, :])
+
+            @pl.when(b == 1)
+            def _():
+                receive(3)
+                load(1, 0).start()
+
+            load(1, 0).wait()
+
+        @pl.when(i == 3)
+        def _():
+            load(1, 1).wait()
 
         cos_t = cos_s.at[b, rows(blk), :]
         sin_t = sin_s.at[b, rows(blk), :]
         trig_t[0] = cos_t[...].T
         trig_t[1] = sin_t[...].T
-        move(1, 0)[-1]().wait()
 
         def late_kv(blk):
             piece = kv_ref.at[b, rows(blk), :]
@@ -433,12 +493,17 @@
 
         @pl.when(i == 2)
         def _():
-            receive_sibling(1)
+            load_relayed(1)
 
         @pl.when((i == 2) & (tp < 2))
         def _():
             late_kv(tp ^ 3).wait_recv()
             transpose_kv(kv_ref, kt_ref, b, True)
+
+        @pl.when(t == 3)
+        def _():
+            for seq in range(NB):
+                take(0, seq, tp ^ 2)
 
         for n in range(1, 5):
             @pl.when(blk == n - 1)
@@ -454,54 +519,21 @@
 
         @pl.when(t == 1)
         def _():
-            weight_grads(False, oqt.at[0, 0], oqt.at[0, 1], buf.at[0], buf.at[1])
+            receive(2)
+            weight_grad(out_acc, False, oqt.at[0, 0], buf.at[1])
+            weight_grad(dwq_acc, False, oqt.at[0, 1], buf.at[0])
             pltpu.make_async_copy(dwq_acc, accq_hbm, lsem.at[9]).start()
             pltpu.make_async_copy(out_acc, acco_hbm, lsem.at[10]).start()
+            finish_dx()
         return carry
 
     lax.fori_loop(0, 4, head_part, 0)
     put_oqt = local(0, oqt.at[0], oqt_hbm)
-    put_out.wait()
-
-    dw_acc[...] = jnp.zeros_like(dw_acc)
-    gain = 1.0 + normw_ref[...]
     put_dkv = []
-
     for b in range(NB):
-        def take(part, blk):
-            piece = dkv_piece(part, b, blk)
-            rc(DKV_X + 2 * part + b, piece, piece, xp).wait_recv()
-            rc(DKV_REL + 2 * part + b, piece, piece, sib).start()
-
-        take(0, tp ^ 2)
-
-        @pl.when(tp < 2)
-        def _():
-            take(1, tp)
-
-        def dx_rows(j, carry):
-            r = pl.ds(pl.multiple_of(b * TB + j * 128, 128), 128)
-            own = pl.ds(pl.multiple_of(tp * TB + j * 128, 128), 128)
-            da = da_acc[r, :] + dot_nt(dkv_ref[0, b, own, :], wkv[...]) + dot_nt(dkv_ref[1, b, own, :], wkv[...])
-            xf = x_ref[r, :].astype(F32)
-            inv = lax.rsqrt(jnp.mean(xf * xf, axis=-1, keepdims=True) + 1e-6)
-            normed = xf * inv
-            prod = da * normed
-            dw_acc[...] += jnp.sum(prod.reshape(-1, *dw_acc.shape), axis=0)
-            corr = jnp.mean(prod * gain, axis=-1, keepdims=True)
-            io_ref[r, :] = (dout_ref[r, :].astype(F32) + inv * (da * gain - normed * corr)).astype(BF16)
-            return carry
-
-        lax.fori_loop(0, 2, dx_rows, 0)
-        if b == NB - 1:
-            dw_parts[0] = jnp.sum(dw_acc[...], axis=0, keepdims=True)
-            put_dx = local(8, io_ref, dx_hbm)
-            start(DW_SIB, dw_parts.at[0], dw_parts.at[1], sib)
-            start(DW_X, dw_parts.at[0], dw_parts.at[2], xp)
-            start(DW_XS, dw_parts.at[0], dw_parts.at[3], xs)
         def arrived(first, part, blk):
             piece = dkv_piece(part, b, blk)
-            rc(first + 2 * part + b, piece, piece, sib).wait_recv()
+            rc(first + NB * part + b, piece, piece, sib).wait_recv()
 
         arrived(DKV_SIB, 0, tp ^ 1)
         arrived(DKV_REL, 0, tp ^ 3)
@@ -517,15 +549,17 @@
         put_dkv.append(local(1 + b, dkv_ref.at[0, b], dkv_hbm.at[0, b]))
         put_dkv.append(local(3 + b, dkv_ref.at[1, b, 0:TOK, :], dkv_hbm.at[1, b, 0:TOK, :]))
 
-    for i in (DW_SIB, DW_X, DW_XS):
-        copies[i].wait_recv()
+    for cp in dw_copies():
+        cp.wait_recv()
     parts = [dw_parts[jnp.bitwise_xor(tp, t)] for t in range(4)]
     dw_ref[...] = sum(parts[1:], parts[0])
 
-    own_a.wait()
-    own_d.wait()
-    for cp in (put_oqt, put_dx, *put_dkv):
+    for cp in (put_oqt, *put_dkv):
         cp.wait()
+    pltpu.make_async_copy(io_ref, dx_hbm, lsem.at[8]).wait()
+    for cp in dw_copies():
+        cp.wait_send()
+    bulk_end().wait_send()
     pltpu.make_async_copy(dwq_acc, accq_hbm, lsem.at[9]).wait()
     pltpu.make_async_copy(out_acc, acco_hbm, lsem.at[10]).wait()
     for i in copies:
@@ -623,7 +657,7 @@
             pltpu.VMEM((2, HW, TOK), BF16),
             pltpu.VMEM((8, D), F32), pltpu.VMEM((4, 1, D), F32),
             pltpu.VMEM((2, TOK, D), BF16),
-            pltpu.SemaphoreType.DMA((N_SEM,)), pltpu.SemaphoreType.DMA((N_SEM,)), pltpu.SemaphoreType.DMA((11,)),
+            pltpu.SemaphoreType.DMA((N_SEM,)), pltpu.SemaphoreType.DMA((N_SEM,)), pltpu.SemaphoreType.DMA((13,)),
         ],
         compiler_params=pltpu.CompilerParams(collective_id=0, has_side_effects=True, vmem_limit_bytes=67_000_000),
         name='main',

time: 158 us -> 157 us (level)
  no operation moved by 1% of the time
where the time goes in v6:
time: 157 us; the launch traced here: 156 us
  Pallas kernels  156 us (99%)
    pallas_call x1, Pallas kernels, local_block(): pl.pallas_call(main_kernel, out_shape=[sds((TOK, D), BF16), sds((TOK, D),...  141 us
    pallas_call x1, Pallas kernels, local_block(): pl.pallas_call(grad_kernel, grid=(steps,), out_shape=[sds((D, HW), F32),...  14.2 us

profile of v6, /device:TPU:0, one launch (start us, length us, event | category | flops | bytes accessed | tf_op | source)
XLA Modules:
  0.0 156.4 jit_solution(1331784440621358821)
XLA Ops:
  0.6 141.4 %main.1 = (bf16[512,2048]{1,0:T(8,128)(2,1)}, bf16[512,2048]{1,0:T(8,128)(2,1)}, f32[1,2048]{1,0:T(1,128)}, f32[512,2048]{1,0:T(8,128)}, f32[512,2048]{1,0:T(8,1...) custom-call(bf16[512,2048]{1,0:T(8,128)(2,1)} %bitcast.6, ...), custom_call_target="tpu_custom_call" | custom-call | tf_op jit(solution)/shard_map/main/pallas_call | solution.py:634
  142.0 14.2 %grads.1 = (f32[2048,512]{1,0:T(8,128)}, f32[512,2048]{1,0:T(8,128)}, f32[2048,128]{1,0:T(8,128)}, f32[2048,128]{1,0:T(8,128)}, bf16[512,2048]{1,0:T(8,128)(2,1)...) custom-call(f32[512,2048]{1,0:T(8,128)} %get-tuple-element.23.accq_ref, f32[512,2048]{1,0:T(8,128)} %get-tuple-element.24.acco_ref, ...), custom_call_target="tpu_custom_call" | custom-call | tf_op jit(solution)/shard_map/grads/pallas_call | solution.py:671

commit v7 on v6

--- a/solution.py
+++ b/solution.py
@@ -82,10 +82,10 @@
 
 
 def main_kernel(x_hbm, dout_hbm, wq_own, wo_own, wk_own, wv_own, normw_ref, pos_ref, freq_ref,
-                out_hbm, dx_hbm, dw_ref, accq_hbm, acco_hbm, oqt_hbm, dkv_hbm, act_all, dout_all,
+                out_hbm, dx_hbm, dw_hbm, accq_hbm, acco_hbm, oqt_hbm, dkv_hbm, act_all, dout_all,
                 x_ref, dout_ref, io_ref, dkv_ref, oqt, trig_t, dwq_acc,
                 act, kv_ref, wkv, cos_s, sin_s, wq_buf, wo_buf, q_s, do_s, o_s, dq_s, out_acc, da_acc, kt_ref,
-                dkv_acc, rs_a, rs_c, dw_acc, dw_parts, buf, send, recv, lsem):
+                dkv_acc, rs_a, rs_c, dw_acc, dw_parts, dw_row, buf, send, recv, lsem):
     dp = lax.axis_index('dp')
     tp = lax.axis_index('tp')
     sib = (dp, tp ^ 1)
@@ -504,6 +504,11 @@
         def _():
             for seq in range(NB):
                 take(0, seq, tp ^ 2)
+            for cp in dw_copies():
+                cp.wait_recv()
+            parts = [dw_parts[jnp.bitwise_xor(tp, d)] for d in range(4)]
+            dw_row[...] = sum(parts[1:], parts[0])
+            pltpu.make_async_copy(dw_row, dw_hbm, lsem.at[5]).start()
 
         for n in range(1, 5):
             @pl.when(blk == n - 1)
@@ -549,14 +554,10 @@
         put_dkv.append(local(1 + b, dkv_ref.at[0, b], dkv_hbm.at[0, b]))
         put_dkv.append(local(3 + b, dkv_ref.at[1, b, 0:TOK, :], dkv_hbm.at[1, b, 0:TOK, :]))
 
-    for cp in dw_copies():
-        cp.wait_recv()
-    parts = [dw_parts[jnp.bitwise_xor(tp, t)] for t in range(4)]
-    dw_ref[...] = sum(parts[1:], parts[0])
-
     for cp in (put_oqt, *put_dkv):
         cp.wait()
     pltpu.make_async_copy(io_ref, dx_hbm, lsem.at[8]).wait()
+    pltpu.make_async_copy(dw_row, dw_hbm, lsem.at[5]).wait()
     for cp in dw_copies():
         cp.wait_send()
     bulk_end().wait_send()
@@ -636,7 +637,7 @@
         out_shape=[sds((TOK, D), BF16), sds((TOK, D), BF16), sds((1, D), F32), sds((HW, D), F32), sds((HW, D), F32),
                    sds((2, HW, TOK), BF16), sds((2, NB, SEQ, 2 * HD), BF16), sds((4, TOK, D), BF16), sds((4, TOK, D), BF16)],
         in_specs=[anym, anym, anym, anym, anym, anym, vmem, vmem, vmem],
-        out_specs=[anym, anym, vmem, anym, anym, anym, anym, anym, anym],
+        out_specs=[anym] * 9,
         scratch_shapes=[
             pltpu.VMEM((TOK, D), BF16), pltpu.VMEM((TOK, D), BF16), pltpu.VMEM((TOK, D), BF16),
             pltpu.VMEM((2, NB, SEQ, 2 * HD), BF16),
@@ -655,7 +656,7 @@
             pltpu.VMEM((NB, SEQ, 2 * HD), F32),
             pltpu.VMEM((2, NB, TB, 2 * HD), F32),
             pltpu.VMEM((2, HW, TOK), BF16),
-            pltpu.VMEM((8, D), F32), pltpu.VMEM((4, 1, D), F32),
+            pltpu.VMEM((8, D), F32), pltpu.VMEM((4, 1, D), F32), pltpu.VMEM((1, D), F32),
             pltpu.VMEM((2, TOK, D), BF16),
             pltpu.SemaphoreType.DMA((N_SEM,)), pltpu.SemaphoreType.DMA((N_SEM,)), pltpu.SemaphoreType.DMA((13,)),
         ],

time: 157 us -> 156 us (level)
  no operation moved by 1% of the time
where the time goes in v7:
time: 156 us
  Pallas kernels  155 us (99%)
    pallas_call x1, Pallas kernels, local_block(): pl.pallas_call(main_kernel, out_shape=[sds((TOK, D), BF16), sds((TOK, D),...  141 us
    pallas_call x1, Pallas kernels, local_block(): pl.pallas_call(grad_kernel, grid=(steps,), out_shape=[sds((D, HW), F32),...  14.2 us

profile of v7, /device:TPU:0, one launch (start us, length us, event | category | flops | bytes accessed | tf_op | source)
XLA Modules:
  0.0 155.9 jit_solution(168790734026813335)
XLA Ops:
  0.6 140.8 %main.1 = (bf16[512,2048]{1,0:T(8,128)(2,1)}, bf16[512,2048]{1,0:T(8,128)(2,1)}, f32[1,2048]{1,0:T(1,128)}, f32[512,2048]{1,0:T(8,128)}, f32[512,2048]{1,0:T(8,1...) custom-call(bf16[512,2048]{1,0:T(8,128)(2,1)} %bitcast.6, ...), custom_call_target="tpu_custom_call" | custom-call | tf_op jit(solution)/shard_map/main/pallas_call | solution.py:635
  141.4 14.2 %grads.1 = (f32[2048,512]{1,0:T(8,128)}, f32[512,2048]{1,0:T(8,128)}, f32[2048,128]{1,0:T(8,128)}, f32[2048,128]{1,0:T(8,128)}, bf16[512,2048]{1,0:T(8,128)(2,1)...) custom-call(f32[512,2048]{1,0:T(8,128)} %get-tuple-element.23.accq_ref, f32[512,2048]{1,0:T(8,128)} %get-tuple-element.24.acco_ref, ...), custom_call_target="tpu_custom_call" | custom-call | tf_op jit(solution)/shard_map/grads/pallas_call | solution.py:672
